TPU v7x, 32 devices: a whole 2x2x4 slice. The times are simulated.
32 devices in a mesh: seq: 16 (over z, x, core), grp: 2 (over y).
Axes of the slice: x: 2, y: 2, z: 4, core: 2. Of those that a mesh axis runs over, the one named last changes fastest.
Arguments:
- out_grad: bfloat16 [2, 3456, 1024], P('grp', 'seq'), may hold values from -6 to 6
- combine_logits: float32 [2, 3456, 64], P('grp', 'seq'), may hold values from -20 to 330
- expert_out: bfloat16 [2, 64, 1024], P('grp', 'seq'), may hold values from -6 to 6
- slot_in: bfloat16 [2, 64, 1024], P('grp', 'seq'), may hold values from -6 to 6
- router: bfloat16 [64, 1024], P('seq'), may hold values from -0.1875 to 0.1875
- w_gate: bfloat16 [64, 2048, 1024], P('seq', 'grp'), may hold values from -0.1875 to 0.1875
- w_up: bfloat16 [64, 2048, 1024], P('seq', 'grp'), may hold values from -0.1875 to 0.1875
- w_down: bfloat16 [64, 2048, 1024], P('seq', 'grp'), may hold values from -0.125 to 0.125
Outputs:
- token_grad: bfloat16 [2, 3456, 1024], P('grp', 'seq')
- slot_grad: float32 [2, 64, 1024], P('grp', 'seq')
- grad_gate: bfloat16 [64, 2048, 1024], P('seq', 'grp')
- grad_up: bfloat16 [64, 2048, 1024], P('seq', 'grp')
- grad_down: bfloat16 [64, 2048, 1024], P('seq', 'grp')
All inputs are finite; a program needn't handle non-finite values.
Results may differ from a plain program's by a relative error of at most 0.028.
Values may be sent and summed in bfloat16 or wider, within the bound.
No kernel may reach another device: no remote copies, remote signals or barrier semaphores. Data moves between devices by JAX's collectives and lax.ppermute only.
A program may use at most 128 MiB of HBM per device.

v0:
```python
import jax
import jax.numpy as jnp
from jax import lax
from jax.sharding import PartitionSpec as P


def slot_backward(inputs, out_grads, w_gate, w_up, w_down):
    gate = jnp.einsum("ged,efd->gef", inputs, w_gate, preferred_element_type=jnp.float32)
    upper = jnp.einsum("ged,efd->gef", inputs, w_up, preferred_element_type=jnp.float32)
    sig = jax.nn.sigmoid(gate)
    hidden = (gate * sig * upper).astype(jnp.bfloat16)
    hidden_grad = jnp.einsum("ged,efd->gef", out_grads, w_down, preferred_element_type=jnp.float32)
    up_grad = (hidden_grad * gate * sig).astype(jnp.bfloat16)
    gate_grad = (hidden_grad * upper * sig * (1.0 + gate * (1.0 - sig))).astype(jnp.bfloat16)
    partial_grad = jnp.einsum("gef,efd->ged", gate_grad, w_gate, preferred_element_type=jnp.float32)
    partial_grad = partial_grad + jnp.einsum(
        "gef,efd->ged", up_grad, w_up, preferred_element_type=jnp.float32
    )
    grad_gate = jnp.einsum(
        "gef,ged->efd", gate_grad, inputs, preferred_element_type=jnp.float32
    ).astype(jnp.bfloat16)
    grad_up = jnp.einsum(
        "gef,ged->efd", up_grad, inputs, preferred_element_type=jnp.float32
    ).astype(jnp.bfloat16)
    grad_down = jnp.einsum(
        "gef,ged->efd", hidden, out_grads, preferred_element_type=jnp.float32
    ).astype(jnp.bfloat16)
    return (partial_grad, grad_gate, grad_up, grad_down)


def per_device(out_grad, combine_logits, expert_out, slot_in, router, w_gate, w_up, w_down):
    grads = out_grad[0]
    probs = jax.nn.softmax(combine_logits[0], axis=-1)
    probs_bf = probs.astype(jnp.bfloat16)
    summed_cols = lax.psum_scatter(
        lax.dot_general(
            grads, probs_bf, (((0,), (0,)), ((), ())), preferred_element_type=jnp.float32
        ).astype(jnp.bfloat16),
        "seq",
        scatter_dimension=0,
        tiled=True,
    )
    owner_cols = lax.all_to_all(summed_cols, "seq", split_axis=1, concat_axis=0, tiled=True)
    slot_out = jnp.transpose(owner_cols)
    weight_grad = lax.dot_general(
        grads,
        lax.all_gather(expert_out[0], "seq", axis=0, tiled=True),
        (((1,), (1,)), ((), ())),
        preferred_element_type=jnp.float32,
    )
    centre = jnp.sum(weight_grad * probs, axis=-1, keepdims=True)
    logit_grad = (probs * (weight_grad - centre)).astype(jnp.bfloat16)
    token_sum = jnp.dot(
        logit_grad,
        lax.all_gather(router, "seq", axis=0, tiled=True),
        preferred_element_type=jnp.float32,
    )
    token_grad = token_sum.astype(jnp.bfloat16)[None]
    all_inputs, all_out = (
        lax.all_gather(slot_in, "grp", axis=0, tiled=True),
        lax.all_gather(slot_out[None], "grp", axis=0, tiled=True),
    )
    partial_grad, grad_gate, grad_up, grad_down = slot_backward(
        all_inputs, all_out, w_gate, w_up, w_down
    )
    slot_grad = lax.psum_scatter(
        partial_grad.astype(jnp.bfloat16), "grp", scatter_dimension=0, tiled=True
    ).astype(jnp.float32)
    return (token_grad, slot_grad, grad_gate, grad_up, grad_down)


def solution(mesh):
    return jax.shard_map(
        per_device,
        mesh=mesh,
        in_specs=(
            P("grp", "seq", None),
            P("grp", "seq", None),
            P("grp", "seq", None),
            P("grp", "seq", None),
            P("seq", None),
            P("seq", "grp", None),
            P("seq", "grp", None),
            P("seq", "grp", None),
        ),
        out_specs=(
            P("grp", "seq", None),
            P("grp", "seq", None),
            P("seq", "grp", None),
            P("seq", "grp", None),
            P("seq", "grp", None),
        ),
        check_vma=False,
    )
```

profile of v0, /device:TPU:0, one launch (start us, length us, event | category | flops | bytes accessed | tf_op | source)
XLA Modules:
  0.0 128.8 jit_solution(1626984013032163660)
XLA Ops:
  7.2 0.0 copy-start
  7.2 0.0 reduce-scatter.4.cloned.1.call-start
  7.2 0.9 reduce_max.9
  8.1 0.9 fusion.11
  9.0 0.0 copy-done
  9.0 1.0 fusion.1
  10.1 0.8 copy.38
  10.9 0.0 reduce-scatter.4.cloned.1.call-update
  10.9 0.0 copy-start.1
  10.9 5.7 %all_gather.15 = bf16[2,4,1024]{2,1,0:T(4,128)(2,1)S(1)} all-gather(bf16[1,4,1024]{2,1,0:T(4,128)(2,1)} %param.11), channel_id=1, replica_groups=mesh['seq'=16,'grp'=2] {'grp'}, dimensions={0}, use_global_device_ids=true | all-gather | bytes 24576 | tf_op jit(solution)/shard_map/all_gather | solution.py:60
  16.6 0.7 copy.29
  17.3 0.0 copy-start.3
  17.4 0.0 copy-start.2
  17.4 0.0 copy-start.4
  17.4 5.7 %convolution_bitcast_fusion = f32[2,4,1024]{2,0,1:T(2,128)S(1)} fusion(bf16[4,1024,1024]{2,1,0:T(8,128)(2,1)} %param.13, bf16[2,4,1024]{2,1,0:T(4,128)(2,1)S(1)} %all_gather.15), kind=kOutput, calls=%fused_computation.8 | convolution fusion | flops 16777216 | bytes 8437760 | tf_op jit(solution)/shard_map/ged,efd->gef/dot_general | solution.py:8
  23.1 0.0 copy-done.1
  23.1 2.3 %convolution_bitcast_fusion.1 = f32[2,4,1024]{2,0,1:T(2,128)S(1)} fusion(bf16[4,1024,1024]{2,1,0:T(8,128)(2,1)S(1)} %copy-done.1, bf16[2,4,1024]{2,1,0:T(4,128)(2,1)S(1)} %all_gather.15), kind=kOutput, calls=%fused_computation.9 | convolution fusion | flops 16777216 | bytes 8437760 | tf_op jit(solution)/shard_map/ged,efd->gef/dot_general | solution.py:9
  25.4 0.0 copy-done.3
  25.4 22.5 %all-gather.2 = bf16[16,4,1024]{2,1,0:T(4,128)(2,1)S(1)} all-gather(bf16[1,4,1024]{2,1,0:T(4,128)(2,1)S(1)} %bitcast.66), channel_id=1, replica_groups=mesh['seq'=16,'grp'=2] {'seq'}, dimensions={0}, use_global_device_ids=true | all-gather | bytes 139264 | tf_op jit(solution)/shard_map/all_gather | solution.py:55
  47.9 18.2 %all-gather = bf16[1,64,1024]{2,0,1:T(2,128)(2,1)S(1)} all-gather(bf16[1,4,1024]{2,0,1:T(2,128)(2,1)S(1)} %copy.29), channel_id=2, replica_groups=mesh['seq'=16,'grp'=2] {'seq'}, dimensions={1}, use_global_device_ids=true | all-gather | bytes 139264 | tf_op jit(solution)/shard_map/all_gather | solution.py:47
  66.2 0.0 copy-done.2
  66.2 0.3 multiply_reduce_fusion
  66.4 4.1 %reduce-scatter.4.cloned.1.call-done = bf16[64,64]{1,0:T(8,128)(2,1)} async-done(((bf16[1024,64]{1,0:T(8,128)(2,1)}), bf16[64,64]{1,0:T(8,128)(2,1)}) %reduce-scatter.4.cloned.1.call-update) | async-done | bytes 8208
  70.6 0.8 copy.39
  71.4 0.7 reshape.35
  72.1 3.7 %all-to-all-start = ((bf16[16,2,128]{2,1,0:T(2,128)(2,1)}), bf16[16,2,128]{2,1,0:T(2,128)(2,1)S(1)}, u32[]{:S(2)}, u32[]{:S(2)}) async-start(bf16[16,2,128]{2,1,0:T(2,128)(2,1)} %reshape.35), calls=%async_computation | async-start | bytes 16384 | tf_op jit(solution)/shard_map/all_to_all | solution.py:43
  75.8 1.1 fusion
  76.9 0.0 copy-done.4
  76.9 0.6 dynamic-slice
  77.5 4.7 %all-to-all-done = bf16[16,2,128]{2,1,0:T(2,128)(2,1)S(1)} async-done(((bf16[16,2,128]{2,1,0:T(2,128)(2,1)}), bf16[16,2,128]{2,1,0:T(2,128)(2,1)S(1)}, u32[]{:S(2)}, u32[]{:S(2)}) %all-to-all-start) | async-done | bytes 8224 | tf_op jit(solution)/shard_map/all_to_all | solution.py:43
  82.2 0.1 reshape.36
  82.3 0.1 all_to_all.17
  82.4 4.5 %all-gather.3 = bf16[2,4,1024]{2,1,0:T(4,128)(2,1)S(1)} all-gather(bf16[1,4,1024]{2,1,0:T(4,128)(2,1)S(1)} %bitcast.65), channel_id=3, replica_groups=mesh['seq'=16,'grp'=2] {'grp'}, dimensions={0}, use_global_device_ids=true | all-gather | bytes 24576 | tf_op jit(solution)/shard_map/all_gather | solution.py:61
  86.9 0.0 slice-start
  86.9 5.8 %convolution_bitcast_fusion.2 = f32[2,4,1024]{2,0,1:T(2,128)S(1)} fusion(bf16[4,1024,1024]{2,1,0:T(8,128)(2,1)} %param.15, bf16[2,4,1024]{2,1,0:T(4,128)(2,1)S(1)} %all-gather.3), kind=kOutput, calls=%fused_computation.10 | convolution fusion | flops 16777216 | bytes 8437760 | tf_op jit(solution)/shard_map/ged,efd->gef/dot_general | solution.py:12
  92.7 0.0 slice-start.1
  92.7 5.8 %convolution_convert_fusion = bf16[4,1024,1024]{2,1,0:T(8,128)(2,1)} fusion(f32[2,4,1024]{2,0,1:T(2,128)S(1)} %convolution_bitcast_fusion.1, f32[2,4,1024]{2,0,1:T(2,128)S(1)} %convolution_bitcast_fusion, bf16[2,4,1024]{2,1,0:T(4,128)(2,1)S(1)} %all-gather.3), kind=kOutput, calls=%fused_computation | convolution fusion | flops 21020672 | bytes 8470528 | tf_op jit(solution)/shard_map/gef,ged->efd/dot_general | solution.py:25
  98.5 0.0 slice-done
  98.5 0.0 slice-done.1
  98.5 0.0 slice-start.2
  98.5 1.2 fusion.22
  99.7 0.0 slice-start.3
  99.7 5.8 %convolution_convert_fusion.2 = bf16[4,1024,1024]{2,1,0:T(8,128)(2,1)} fusion(bf16[2,4,1024]{2,1,0:T(4,128)(2,1)S(1)} %all_gather.15, f32[2,4,1024]{2,0,1:T(2,128)S(1)} %convolution_bitcast_fusion, f32[2,4,1024]{2,0,1:T(2,128)S(1)} %convolution_bitcast_fusion.2, f32[2,4,1024]{2,0,1:T(2,128)S(1)} %convolution_bitcast_fusion.1), kind=kOutput, calls=%fused_computation.2 | convolution fusion | flops 21053440 | bytes 8503296 | tf_op jit(solution)/shard_map/gef,ged->efd/dot_general | solution.py:19
  105.6 5.8 %convolution_convert_fusion.1 = bf16[4,1024,1024]{2,1,0:T(8,128)(2,1)} fusion(bf16[2,4,1024]{2,1,0:T(4,128)(2,1)S(1)} %all_gather.15, f32[2,4,1024]{2,0,1:T(2,128)S(1)} %convolution_bitcast_fusion.2, f32[2,4,1024]{2,0,1:T(2,128)S(1)} %convolution_bitcast_fusion), kind=kOutput, calls=%fused_computation.1 | convolution fusion | flops 21020672 | bytes 8470528 | tf_op jit(solution)/shard_map/gef,ged->efd/dot_general | solution.py:22
  111.4 0.0 slice-done.2
  111.4 0.0 slice-done.3
  111.4 1.2 fusion.3
  112.6 8.1 %all-reduce = bf16[2,4,1024]{2,1,0:T(4,128)(2,1)S(1)} all-reduce(bf16[2,4,1024]{2,1,0:T(4,128)(2,1)S(1)} %copy.34), channel_id=5, replica_groups=mesh['seq'=16,'grp'=2] {'grp'}, use_global_device_ids=true, to_apply=%region_4.0.clone | all-reduce | flops 8192 | bytes 32768
  120.7 1.2 dynamic-slice_convert_fusion
  (6 shorter events, 0.1 us)
Async XLA Ops:
  7.2 1.8 %copy-start = (bf16[1,216,1024]{2,1,0:T(8,128)(2,1)S(1)}, bf16[1,216,1024]{2,1,0:T(8,128)(2,1)}, u32[]{:S(2)}) copy-start(bf16[1,216,1024]{2,1,0:T(8,128)(2,1)} %param.8) | copy-start | bytes 1327108
  7.2 63.4 %reduce-scatter.4.cloned.1.call-start = ((), (), s32[]{:S(2)}) async-start(), calls=%async_computation.2 | async-start | bytes 278528
  10.9 12.1 %copy-start.1 = (bf16[4,1024,1024]{2,1,0:T(8,128)(2,1)S(1)}, bf16[4,1024,1024]{2,1,0:T(8,128)(2,1)}, u32[]{:S(2)}) copy-start(bf16[4,1024,1024]{2,1,0:T(8,128)(2,1)} %param.14) | copy-start | bytes 25165828
  17.3 8.0 %copy-start.3 = (bf16[4,1024]{1,0:T(4,128)(2,1)S(1)}, bf16[4,1024]{1,0:T(4,128)(2,1)}, u32[]{:S(2)}) copy-start(bf16[4,1024]{1,0:T(4,128)(2,1)} %param.12) | copy-start | bytes 24580
  17.4 48.8 %copy-start.2 = (f32[1,216,64]{1,2,0:T(8,128)S(1)}, f32[1,216,64]{1,2,0:T(8,128)}, u32[]{:S(2)}) copy-start(f32[1,216,64]{1,2,0:T(8,128)} %param.9) | copy-start | bytes 165892
  17.4 59.5 %copy-start.4 = (u32[32]{0:T(128)S(1)}, u32[32]{0:T(128)}, u32[]{:S(2)}) copy-start(u32[32]{0:T(128)} %constant.17) | copy-start | bytes 388
  72.1 10.1 %all-to-all-start = ((bf16[16,2,128]{2,1,0:T(2,128)(2,1)}), bf16[16,2,128]{2,1,0:T(2,128)(2,1)S(1)}, u32[]{:S(2)}, u32[]{:S(2)}) async-start(bf16[16,2,128]{2,1,0:T(2,128)(2,1)} %reshape.35), calls=%async_computation | async-start | bytes 16384 | tf_op jit(solution)/shard_map/all_to_all | solution.py:43
  86.9 11.6 %slice-start = ((s8[8388608]{0:T(1024)(128)(4,1)}), s8[4194304]{0:T(1024)(128)(4,1)S(1)}, s32[]{:S(2)}) async-start(s8[8388608]{0:T(1024)(128)(4,1)} %bitcast.60), calls=%async_computation.3 | async-start | bytes 8388608
  92.7 5.8 %slice-start.1 = ((s8[8388608]{0:T(1024)(128)(4,1)}), s8[4194304]{0:T(1024)(128)(4,1)S(1)}, s32[]{:S(2)}) async-start(s8[8388608]{0:T(1024)(128)(4,1)} %bitcast.60), calls=%async_computation.4 | async-start | bytes 8388608
  98.5 12.8 %slice-start.2 = ((s8[8388608]{0:T(1024)(128)(4,1)}), s8[4194304]{0:T(1024)(128)(4,1)S(1)}, s32[]{:S(2)}) async-start(s8[8388608]{0:T(1024)(128)(4,1)} %bitcast.62), calls=%async_computation.5 | async-start | bytes 8388608
  99.7 11.6 %slice-start.3 = ((s8[8388608]{0:T(1024)(128)(4,1)}), s8[4194304]{0:T(1024)(128)(4,1)S(1)}, s32[]{:S(2)}) async-start(s8[8388608]{0:T(1024)(128)(4,1)} %bitcast.62), calls=%async_computation.6 | async-start | bytes 8388608
Sparse Core Ops, SparseCore 0:
  12.1 58.4 reduce-scatter.3
where the time goes:
time: 129 us
  blocking collectives  59.1 us (46%)
  matrix products  36 us (28%)
  between operations  14.1 us (11%)
  waiting for transfers between devices  8.83 us (7%)
  local copies, waits for them, and re-layouts  3.92 us (3%)
  starting transfers between devices  3.78 us (3%)
  other arithmetic  3.01 us (2%)
    all_gather x1, blocking collectives, per_device(): lax.all_gather(router, 'seq', axis=0, tiled=True)  22.5 us
    all_gather x1, blocking collectives, per_device(): lax.all_gather(expert_out[0], 'seq', axis=0, tiled=True)  18.2 us
    unnamed x1, blocking collectives  8.14 us
    dot_general x1, matrix products, slot_backward(): jnp.einsum('gef,ged->efd', hidden, out_grads, preferred_element_type=jnp....  5.82 us
    dot_general x1, matrix products, slot_backward(): jnp.einsum('gef,ged->efd', gate_grad, inputs, preferred_element_type=jnp....  5.82 us
    dot_general x1, matrix products, slot_backward(): jnp.einsum('gef,ged->efd', up_grad, inputs, preferred_element_type=jnp.fl...  5.81 us
    dot_general x1, matrix products, slot_backward(): jnp.einsum('ged,efd->gef', out_grads, w_down, preferred_element_type=jnp....  5.79 us
    dot_general x1, matrix products, slot_backward(): jnp.einsum('ged,efd->gef', inputs, w_gate, preferred_element_type=jnp.flo...  5.69 us
  transfers between devices with their start and end apart: 2, of which 2 were waited for; matrix products, arithmetic and copies ran while one was open for 8% of the time, Pallas kernels for 0%

commit v1 on v0

v1 whole, which is shorter than its diff:
```python
import jax
import jax.numpy as jnp
from jax import lax
from jax.sharding import PartitionSpec as P

F32 = jnp.float32
BF16 = jnp.bfloat16


def shifted(x, size, k):
    return lax.ppermute(x, "grp", [((i + k) % size, i) for i in range(size)])


def slot_backward(inputs, out_grads, w_gate, w_up, w_down):
    gate = jnp.einsum("ged,efd->gef", inputs, w_gate, preferred_element_type=F32)
    upper = jnp.einsum("ged,efd->gef", inputs, w_up, preferred_element_type=F32)
    sig = jax.nn.sigmoid(gate)
    hidden = (gate * sig * upper).astype(BF16)
    hidden_grad = jnp.einsum("ged,efd->gef", out_grads, w_down, preferred_element_type=F32)
    up_grad = (hidden_grad * gate * sig).astype(BF16)
    gate_grad = (hidden_grad * upper * sig * (1.0 + gate * (1.0 - sig))).astype(BF16)
    partial_grad = jnp.einsum("gef,efd->ged", gate_grad, w_gate, preferred_element_type=F32)
    partial_grad = partial_grad + jnp.einsum("gef,efd->ged", up_grad, w_up, preferred_element_type=F32)
    grad_gate = jnp.einsum("gef,ged->efd", gate_grad, inputs, preferred_element_type=F32).astype(BF16)
    grad_up = jnp.einsum("gef,ged->efd", up_grad, inputs, preferred_element_type=F32).astype(BF16)
    grad_down = jnp.einsum("gef,ged->efd", hidden, out_grads, preferred_element_type=F32).astype(BF16)
    return partial_grad, grad_gate, grad_up, grad_down


def per_device(n_seq, n_grp, out_grad, combine_logits, expert_out, slot_in, router, w_gate, w_up, w_down):
    grads = out_grad[0]
    own, width = router.shape
    inputs = jnp.stack([slot_in[0]] + [shifted(slot_in[0], n_grp, k) for k in range(1, n_grp)])
    probs = jax.nn.softmax(combine_logits[0], axis=-1)
    partial = lax.dot_general(probs.astype(BF16), grads, (((0,), (0,)), ((), ())), preferred_element_type=F32)
    parts = lax.all_to_all(
        partial.astype(BF16).reshape(n_seq, own, width), "seq", split_axis=0, concat_axis=0, tiled=True
    )
    mine = jnp.concatenate([expert_out[0], router], axis=0)
    every = lax.all_to_all(
        jnp.broadcast_to(mine[None], (n_seq, 2 * own, width)), "seq", split_axis=0, concat_axis=0, tiled=True
    )
    outputs = every[:, :own].reshape(n_seq * own, width)
    routers = every[:, own:].reshape(n_seq * own, width)
    weight_grad = lax.dot_general(grads, outputs, (((1,), (1,)), ((), ())), preferred_element_type=F32)
    centre = jnp.sum(weight_grad * probs, axis=-1, keepdims=True)
    logit_grad = (probs * (weight_grad - centre)).astype(BF16)
    token_grad = jnp.dot(logit_grad, routers, preferred_element_type=F32).astype(BF16)[None]
    slot_out = jnp.sum(parts.astype(F32), axis=0).astype(BF16)
    all_out = jnp.stack([slot_out] + [shifted(slot_out, n_grp, k) for k in range(1, n_grp)])
    partial_grad, grad_gate, grad_up, grad_down = slot_backward(inputs, all_out, w_gate, w_up, w_down)
    slot_grad = partial_grad[0]
    for k in range(1, n_grp):
        slot_grad = slot_grad + shifted(partial_grad[k].astype(BF16), n_grp, n_grp - k).astype(F32)
    return token_grad, slot_grad[None], grad_gate, grad_up, grad_down


def solution(mesh):
    def body(*args):
        return per_device(mesh.shape["seq"], mesh.shape["grp"], *args)

    tokens, weights = P("grp", "seq", None), P("seq", "grp", None)
    return jax.shard_map(
        body,
        mesh=mesh,
        in_specs=(tokens, tokens, tokens, tokens, P("seq", None), weights, weights, weights),
        out_specs=(tokens, tokens, weights, weights, weights),
        check_vma=False,
    )
```

time: 129 us -> 63.6 us (0.49)
  blocking collectives: 59.1 us -> 0 us
  between operations: 14.1 us -> 0.79 us
  starting transfers between devices: 3.78 us -> 16.6 us
  waiting for transfers between devices: 8.83 us -> 0.79 us
  matrix products: 36 us -> 39.3 us
  local copies, waits for them, and re-layouts: 3.92 us -> 2.44 us
    all_gather x4 -> x0, blocking collectives: 51 us -> none  [the longest x1 22.5 us: per_device(): lax.all_gather(router, 'seq', axis=0, tiled=True)]
    unnamed x1 -> x0, blocking collectives: 8.14 us -> none
    all_to_all x1 -> x2, starting transfers between devices: 3.74 us -> 11.3 us  [the longest x1 5.91 us: per_device(): lax.all_to_all(partial.astype(BF16).reshape(n_seq, own, width), 'seq', sp...]
    ppermute x0 -> x3, starting transfers between devices: none -> 5.21 us  [shifted(): return lax.ppermute(x, 'grp', [((i + k) % size, i) for i in range(size)])]
    unnamed x2 -> x0, waiting for transfers between devices: 4.14 us -> none
    all_to_all x1 -> x2, waiting for transfers between devices: 4.69 us -> 0.78 us  [the longest x1 0.78 us: per_device(): lax.all_to_all(partial.astype(BF16).reshape(n_seq, own, width), 'seq', sp...]
    dot_general x11, matrix products: 36 us -> 39.3 us  [the longest x1 5.82 us: slot_backward(): jnp.einsum('gef,ged->efd', hidden, out_grads, preferred_element_type=F32)]
    unnamed x25 -> x14, local copies, waits for them, and re-layouts: 3.81 us -> 0.75 us
  transfers between devices with their start and end apart: 2 -> 5, of which waited for: 2 -> 1; matrix products, arithmetic and copies ran while one was open for 8% -> 68% of each run, Pallas kernels for 0% -> 0%
where the time goes in v1:
time: 63.6 us; the launch traced here: 63 us
  matrix products  39.3 us (62%)
  starting transfers between devices  16.6 us (26%)
  other arithmetic  3.15 us (5%)
  local copies, waits for them, and re-layouts  2.44 us (4%)
  waiting for transfers between devices  0.79 us (1%)
  between operations  0.79 us (1%)
    all_to_all x1, starting transfers between devices, per_device(): lax.all_to_all(partial.astype(BF16).reshape(n_seq, own, width), 'seq', sp...  5.91 us
    dot_general x1, matrix products, slot_backward(): jnp.einsum('gef,ged->efd', hidden, out_grads, preferred_element_type=F32)  5.82 us
    dot_general x1, matrix products, slot_backward(): jnp.einsum('gef,ged->efd', gate_grad, inputs, preferred_element_type=F32)  5.82 us
    dot_general x1, matrix products, slot_backward(): jnp.einsum('gef,ged->efd', up_grad, inputs, preferred_element_type=F32)  5.81 us
    dot_general x1, matrix products, slot_backward(): jnp.einsum('ged,efd->gef', out_grads, w_down, preferred_element_type=F32)  5.79 us
    dot_general x1, matrix products, slot_backward(): jnp.einsum('ged,efd->gef', inputs, w_gate, preferred_element_type=F32)  5.64 us
    dot_general x1, matrix products, slot_backward(): upper = jnp.einsum('ged,efd->gef', inputs, w_up, preferred_element_type=F32)  5.64 us
    all_to_all x1, starting transfers between devices, per_device(): lax.all_to_all(jnp.broadcast_to(mine[None], (n_seq, 2 * own, width)), 'se...  5.43 us
  transfers between devices with their start and end apart: 5, of which 1 were waited for; matrix products, arithmetic and copies ran while one was open for 68% of the time, Pallas kernels for 0%

profile of v1, /device:TPU:0, one launch (start us, length us, event | category | flops | bytes accessed | tf_op | source)
XLA Modules:
  0.0 63.0 jit_solution(11281744825853966711)
XLA Ops:
  0.6 0.0 copy-start
  0.6 3.1 %collective-permute-start.1 = (bf16[4,1024]{1,0:T(4,128)(2,1)}, bf16[4,1024]{1,0:T(4,128)(2,1)S(1)}, u32[]{:S(2)}, u32[]{:S(2)}) collective-permute-start(bf16[4,1024]{1,0:T(4,128)(2,1)} %bitcast.61), channel_id=1, source_target_pairs={{1,0},{0,1},{3,2},{2,3},{5,4},{4,5},{7,6},{6,7},{9,8},{8,9},{11,10... | collective-permute-start | bytes 24584 | tf_op jit(solution)/shard_map/ppermute | solution.py:11
  3.7 0.9 %reduce_max.9 = f32[216]{0:T(256)S(1)} reduce(f32[1,216,64]{1,2,0:T(8,128)} %param.9, f32[]{:T(128)} %constant.1.clone.1), dimensions={0,2}, to_apply=%region_0.0 | reduce | flops 13608 | bytes 56164 | tf_op jit(solution)/shard_map/reduce_max | solution.py:34
  4.6 0.9 %fusion.6 = f32[216]{0:T(256)S(1)} fusion(f32[1,216,64]{1,2,0:T(8,128)} %param.9, f32[216]{0:T(256)S(1)} %reduce_max.9), kind=kLoop, calls=%fused_computation.20 | loop fusion | flops 27432 | bytes 57024 | tf_op jit(solution)/shard_map/reduce_sum | solution.py:34
  5.4 0.0 copy-done
  5.5 1.0 %convolution_convert_fusion.4 = bf16[64,1024]{1,0:T(8,128)(2,1)S(1)} fusion(bf16[1,216,1024]{2,1,0:T(8,128)(2,1)S(1)} %copy-done, f32[1,216,64]{1,2,0:T(8,128)} %param.9, f32[216]{0:T(256)S(1)} %fusion.6, f32[216]{0:T(256)S(1)} %reduce_max.9), kind=kOutput, calls=%fused_computation.5 | convolution fusion | flops 28418560 | bytes 630464 | tf_op jit(solution)/shard_map/dot_general | solution.py:35
  6.5 0.7 %reshape.35 = bf16[16,4,1024]{2,1,0:T(4,128)(2,1)} reshape(bf16[64,1024]{1,0:T(8,128)(2,1)S(1)} %convolution_convert_fusion.4) | data formatting | bytes 262144 | tf_op jit(solution)/shard_map/reshape | solution.py:37
  7.2 5.9 %all-to-all-start.1 = ((bf16[16,4,1024]{2,1,0:T(4,128)(2,1)}), bf16[16,4,1024]{2,1,0:T(4,128)(2,1)S(1)}, u32[]{:S(2)}, u32[]{:S(2)}) async-start(bf16[16,4,1024]{2,1,0:T(4,128)(2,1)} %reshape.35), calls=%async_computation.1 | async-start | bytes 262144 | tf_op jit(solution)/shard_map/all_to_all | solution.py:36
  13.1 0.7 %pad_maximum_fusion = bf16[8,1024]{1,0:T(8,128)(2,1)S(1)} fusion(bf16[4,1024]{1,0:T(4,128)(2,1)} %param.12, bf16[4,1024]{1,0:T(4,128)(2,1)} %bitcast.65), kind=kLoop, calls=%fused_computation.29 | loop fusion | flops 32768 | bytes 32768 | tf_op jit(solution)/shard_map/concatenate | solution.py:39
  13.9 0.7 %copy.21 = bf16[1,4,1024]{2,0,1:T(2,128)(2,1)S(1)} copy(bf16[1,4,1024]{2,1,0:T(4,128)(2,1)} %param.11) | data formatting | bytes 16384 | tf_op args[3]
  14.6 0.0 collective-permute-done.1
  14.6 5.6 %convolution_bitcast_fusion.1 = f32[2,4,1024]{2,0,1:T(2,128)S(1)} fusion(bf16[4,1024,1024]{2,1,0:T(8,128)(2,1)} %param.13, bf16[1,4,1024]{2,0,1:T(2,128)(2,1)S(1)} %copy.22, bf16[1,4,1024]{2,0,1:T(2,128)(2,1)S(1)} %copy.21), kind=kOutput, calls=%fused_computation.9 | convolution fusion | flops 16809984 | bytes 8437760 | tf_op jit(solution)/shard_map/ged,efd->gef/dot_general | solution.py:15
  20.3 0.8 %all-to-all-done.1 = bf16[16,4,1024]{2,1,0:T(4,128)(2,1)S(1)} async-done(((bf16[16,4,1024]{2,1,0:T(4,128)(2,1)}), bf16[16,4,1024]{2,1,0:T(4,128)(2,1)S(1)}, u32[]{:S(2)}, u32[]{:S(2)}) %all-to-all-start.1) | async-done | bytes 131104 | tf_op jit(solution)/shard_map/all_to_all | solution.py:36
  21.0 0.7 %broadcast_in_dim.6 = bf16[16,8,1024]{2,1,0:T(8,128)(2,1)} broadcast(bf16[8,1024]{1,0:T(8,128)(2,1)S(1)} %pad_maximum_fusion), dimensions={1,2} | broadcast | bytes 278528 | tf_op jit(solution)/shard_map/broadcast_in_dim | solution.py:41
  21.8 5.4 %all-to-all-start = ((bf16[16,8,1024]{2,1,0:T(8,128)(2,1)}), bf16[16,8,1024]{2,1,0:T(8,128)(2,1)S(1)}, u32[]{:S(2)}, u32[]{:S(2)}) async-start(bf16[16,8,1024]{2,1,0:T(8,128)(2,1)} %broadcast_in_dim.6), calls=%async_computation | async-start | bytes 524288 | tf_op jit(solution)/shard_map/all_to_all | solution.py:40
  27.2 0.1 reduce_sum.32
  27.3 0.6 collective-permute-start
  27.8 5.6 %convolution_bitcast_fusion.2 = f32[2,4,1024]{2,0,1:T(2,128)S(1)} fusion(bf16[4,1024,1024]{2,1,0:T(8,128)(2,1)} %param.14, bf16[1,4,1024]{2,0,1:T(2,128)(2,1)S(1)} %copy.22, bf16[1,4,1024]{2,0,1:T(2,128)(2,1)S(1)} %copy.21), kind=kOutput, calls=%fused_computation.10 | convolution fusion | flops 16809984 | bytes 8437760 | tf_op jit(solution)/shard_map/ged,efd->gef/dot_general | solution.py:16
  33.5 0.0 collective-permute-done
  33.5 0.0 slice-start
  33.6 5.8 %convolution_bitcast_fusion.3 = f32[2,4,1024]{2,0,1:T(2,128)S(1)} fusion(bf16[4,1024,1024]{2,1,0:T(8,128)(2,1)} %param.15, bf16[1,4,1024]{2,0,1:T(2,128)(2,1)S(1)} %copy.20, bf16[1,4,1024]{2,0,1:T(2,128)(2,1)S(1)} %copy.19), kind=kOutput, calls=%fused_computation.11 | convolution fusion | flops 16809984 | bytes 8437760 | tf_op jit(solution)/shard_map/ged,efd->gef/dot_general | solution.py:19
  39.4 0.0 slice-start.1
  39.4 5.8 %convolution_convert_fusion = bf16[4,1024,1024]{2,1,0:T(8,128)(2,1)} fusion(f32[2,4,1024]{2,0,1:T(2,128)S(1)} %convolution_bitcast_fusion.2, f32[2,4,1024]{2,0,1:T(2,128)S(1)} %convolution_bitcast_fusion.1, bf16[1,4,1024]{2,0,1:T(2,128)(2,1)S(1)} %copy.20, bf16[1,4,1024]{2,0,1:T(2,128)(2,1)S(1)} %copy.19), kind=kOutput, calls=%fused_computation | convolution fusion | flops 21053440 | bytes 8470528 | tf_op jit(solution)/shard_map/gef,ged->efd/dot_general | solution.py:26
  45.2 0.0 slice-done
  45.2 0.0 slice-done.1
  45.2 0.0 slice-start.2
  45.2 1.2 %fusion.12 = f32[4,2,1024]{2,1,0:T(2,128)S(1)} fusion(bf16[4,1024,1024]{2,1,0:T(8,128)(2,1)S(1)} %bitcast.57, f32[2,4,1024]{2,0,1:T(2,128)S(1)} %convolution_bitcast_fusion.1, f32[2,4,1024]{2,0,1:T(2,128)S(1)} %convolution_bitcast_fusion.3, f32[2,4,1024]{2,0,1:T(2,128)S(1)} %convolution_bitcast_fusion.2), kind=kOutput, calls=%fused_computation.35 | convolution fusion | flops 16859136 | bytes 8519680 | tf_op jit(solution)/shard_map/gef,efd->ged/dot_general | solution.py:22
  46.4 0.0 slice-start.3
  46.4 5.8 %convolution_convert_fusion.2 = bf16[4,1024,1024]{2,1,0:T(8,128)(2,1)} fusion(f32[2,4,1024]{2,0,1:T(2,128)S(1)} %convolution_bitcast_fusion.1, f32[2,4,1024]{2,0,1:T(2,128)S(1)} %convolution_bitcast_fusion.3, f32[2,4,1024]{2,0,1:T(2,128)S(1)} %convolution_bitcast_fusion.2, bf16[1,4,1024]{2,0,1:T(2,128)(2,1)S(1)} %copy.22, bf16[1,4,1024]{2,0,1:T(2,128)(2,1)S(1)} %copy.21), kind=kOutput, calls=%fused_computation.2 | convolution fusion | flops 21086208 | bytes 8503296 | tf_op jit(solution)/shard_map/gef,ged->efd/dot_general | solution.py:24
  52.2 0.0 slice-done.2
  52.2 0.0 slice-done.3
  52.2 0.0 copy-start.1
  52.2 1.2 %fusion.1 = f32[2,4,1024]{2,0,1:T(2,128)S(1)} fusion(f32[4,2,1024]{2,1,0:T(2,128)S(1)} %fusion.12, bf16[4,1024,1024]{2,1,0:T(8,128)(2,1)S(1)} %bitcast.59, f32[2,4,1024]{2,0,1:T(2,128)S(1)} %convolution_bitcast_fusion.3, f32[2,4,1024]{2,0,1:T(2,128)S(1)} %convolution_bitcast_fusion.1), kind=kOutput, calls=%fused_computation.8 | convolution fusion | flops 16834560 | bytes 8519680 | tf_op jit(solution)/shard_map/gef,efd->ged/dot_general | solution.py:23
  53.5 1.6 %collective-permute-start.2 = (bf16[4,1024]{1,0:T(4,128)(2,1)S(1)}, bf16[4,1024]{1,0:T(4,128)(2,1)S(1)}, u32[]{:S(2)}, u32[]{:S(2)}) collective-permute-start(bf16[4,1024]{1,0:T(4,128)(2,1)S(1)} %bitcast.63), channel_id=1, source_target_pairs={{1,0},{0,1},{3,2},{2,3},{5,4},{4,5},{7,6},{6,7},{9,8},{8,9},{11,10... | collective-permute-start | bytes 24584 | tf_op jit(solution)/shard_map/ppermute | solution.py:11
  55.0 5.8 %convolution_convert_fusion.1 = bf16[4,1024,1024]{2,1,0:T(8,128)(2,1)} fusion(f32[2,4,1024]{2,0,1:T(2,128)S(1)} %convolution_bitcast_fusion.3, f32[2,4,1024]{2,0,1:T(2,128)S(1)} %convolution_bitcast_fusion.1, bf16[1,4,1024]{2,0,1:T(2,128)(2,1)S(1)} %copy.22, bf16[1,4,1024]{2,0,1:T(2,128)(2,1)S(1)} %copy.21), kind=kOutput, calls=%fused_computation.1 | convolution fusion | flops 21053440 | bytes 8470528 | tf_op jit(solution)/shard_map/gef,ged->efd/dot_general | solution.py:25
  60.9 0.0 collective-permute-done.2
  60.9 0.6 fusion.11
  61.5 0.0 all-to-all-done
  61.5 0.1 fusion.13
  61.6 0.0 copy-done.1
  61.6 0.3 multiply_reduce_fusion
  62.0 1.1 %fusion = bf16[1,216,1024]{2,1,0:T(8,128)(2,1)} fusion(bf16[64,1024]{1,0:T(8,128)(2,1)S(1)} %reshape.34, f32[216,64]{0,1:T(8,128)S(1)} %get-tuple-element.8, f32[216]{0:T(256)S(1)} %get-tuple-element.7, f32[1,216,64]{1,2,0:T(8,128)S(1)} %copy-done.1, f32[216]{0:T(256)S(1)} %fusion.6, f32[216]{0:T(256)S(1)} %reduce_max.9), kind=kOutput, calls=%fused_computation.4 | convolution fusion | flops 28601856 | bytes 686624 | tf_op jit(solution)/shard_map/dot_general | solution.py:48
  (10 shorter events, 0.2 us)
Async XLA Ops:
  0.6 4.8 %copy-start = (bf16[1,216,1024]{2,1,0:T(8,128)(2,1)S(1)}, bf16[1,216,1024]{2,1,0:T(8,128)(2,1)}, u32[]{:S(2)}) copy-start(bf16[1,216,1024]{2,1,0:T(8,128)(2,1)} %param.8) | copy-start | bytes 1327108
  0.6 13.9 %collective-permute-start.1 = (bf16[4,1024]{1,0:T(4,128)(2,1)}, bf16[4,1024]{1,0:T(4,128)(2,1)S(1)}, u32[]{:S(2)}, u32[]{:S(2)}) collective-permute-start(bf16[4,1024]{1,0:T(4,128)(2,1)} %bitcast.61), channel_id=1, source_target_pairs={{1,0},{0,1},{3,2},{2,3},{5,4},{4,5},{7,6},{6,7},{9,8},{8,9},{11,10... | collective-permute-start | bytes 24584 | tf_op jit(solution)/shard_map/ppermute | solution.py:11
  7.2 13.8 %all-to-all-start.1 = ((bf16[16,4,1024]{2,1,0:T(4,128)(2,1)}), bf16[16,4,1024]{2,1,0:T(4,128)(2,1)S(1)}, u32[]{:S(2)}, u32[]{:S(2)}) async-start(bf16[16,4,1024]{2,1,0:T(4,128)(2,1)} %reshape.35), calls=%async_computation.1 | async-start | bytes 262144 | tf_op jit(solution)/shard_map/all_to_all | solution.py:36
  21.8 39.7 %all-to-all-start = ((bf16[16,8,1024]{2,1,0:T(8,128)(2,1)}), bf16[16,8,1024]{2,1,0:T(8,128)(2,1)S(1)}, u32[]{:S(2)}, u32[]{:S(2)}) async-start(bf16[16,8,1024]{2,1,0:T(8,128)(2,1)} %broadcast_in_dim.6), calls=%async_computation | async-start | bytes 524288 | tf_op jit(solution)/shard_map/all_to_all | solution.py:40
  27.3 6.2 %collective-permute-start = (bf16[4,1024]{1,0:T(4,128)(2,1)S(1)}, bf16[4,1024]{1,0:T(4,128)(2,1)S(1)}, u32[]{:S(2)}, u32[]{:S(2)}) collective-permute-start(bf16[4,1024]{1,0:T(4,128)(2,1)S(1)} %reduce_sum.32), channel_id=1, source_target_pairs={{1,0},{0,1},{3,2},{2,3},{5,4},{4,5},{7,6},{6,7},{9,8},{8,9},{11,10... | collective-permute-start | bytes 24584 | tf_op jit(solution)/shard_map/ppermute | solution.py:11
  33.5 11.6 %slice-start = ((s8[8388608]{0:T(1024)(128)(4,1)}), s8[4194304]{0:T(1024)(128)(4,1)S(1)}, s32[]{:S(2)}) async-start(s8[8388608]{0:T(1024)(128)(4,1)} %bitcast.56), calls=%async_computation.2 | async-start | bytes 8388608
  39.4 5.8 %slice-start.1 = ((s8[8388608]{0:T(1024)(128)(4,1)}), s8[4194304]{0:T(1024)(128)(4,1)S(1)}, s32[]{:S(2)}) async-start(s8[8388608]{0:T(1024)(128)(4,1)} %bitcast.56), calls=%async_computation.3 | async-start | bytes 8388608
  45.2 7.0 %slice-start.2 = ((s8[8388608]{0:T(1024)(128)(4,1)}), s8[4194304]{0:T(1024)(128)(4,1)S(1)}, s32[]{:S(2)}) async-start(s8[8388608]{0:T(1024)(128)(4,1)} %bitcast.58), calls=%async_computation.4 | async-start | bytes 8388608
  46.4 5.8 %slice-start.3 = ((s8[8388608]{0:T(1024)(128)(4,1)}), s8[4194304]{0:T(1024)(128)(4,1)S(1)}, s32[]{:S(2)}) async-start(s8[8388608]{0:T(1024)(128)(4,1)} %bitcast.58), calls=%async_computation.5 | async-start | bytes 8388608
  52.2 9.4 %copy-start.1 = (f32[1,216,64]{1,2,0:T(8,128)S(1)}, f32[1,216,64]{1,2,0:T(8,128)}, u32[]{:S(2)}) copy-start(f32[1,216,64]{1,2,0:T(8,128)} %param.9) | copy-start | bytes 165892
  53.5 7.4 %collective-permute-start.2 = (bf16[4,1024]{1,0:T(4,128)(2,1)S(1)}, bf16[4,1024]{1,0:T(4,128)(2,1)S(1)}, u32[]{:S(2)}, u32[]{:S(2)}) collective-permute-start(bf16[4,1024]{1,0:T(4,128)(2,1)S(1)} %bitcast.63), channel_id=1, source_target_pairs={{1,0},{0,1},{3,2},{2,3},{5,4},{4,5},{7,6},{6,7},{9,8},{8,9},{11,10... | collective-permute-start | bytes 24584 | tf_op jit(solution)/shard_map/ppermute | solution.py:11

commit v2 on v1

v2 whole, which is shorter than its diff:
```python
import functools

import jax
import jax.numpy as jnp
from jax import lax
from jax.experimental import pallas as pl
from jax.experimental.pallas import tpu as pltpu
from jax.sharding import PartitionSpec as P

F32 = jnp.float32
BF16 = jnp.bfloat16
VMEM = pl.BlockSpec(memory_space=pltpu.VMEM)
HBM = pl.BlockSpec(memory_space=pltpu.HBM)
SEMS = pltpu.SemaphoreType.DMA


def shape(dims, kind):
    return jax.ShapeDtypeStruct(dims, kind)


def in_hbm(x):
    return pltpu.with_memory_space_constraint(x, pltpu.HBM)


def dot(a, b, contract):
    return lax.dot_general(a, b, (contract, ((), ())), preferred_element_type=F32)


def start(src, dst, sem):
    copy = pltpu.make_async_copy(src, dst, sem)
    copy.start()
    return copy


def call(body, name, outs, out_specs, args, in_specs, scratch=(), us=1.0, vmem=8 << 20):
    return pl.pallas_call(
        body,
        name=name,
        out_shape=outs,
        in_specs=in_specs,
        out_specs=out_specs,
        scratch_shapes=scratch,
        compiler_params=pltpu.CompilerParams(vmem_limit_bytes=vmem),
        cost_estimate=pl.CostEstimate(flops=int(us * 8e8), bytes_accessed=int(us * 3e6), transcendentals=0),
    )(*args)


def soft_kernel(logits_hbm, grads_hbm, outputs_hbm, router_hbm, x_hbm, probs_ref, all_hbm, x_ref,
                logits_ref, grads_ref, both_ref, parts_ref, sems, both_sems, parts_sems):
    loads = [
        start(outputs_hbm, both_ref.at[0], sems.at[2]),
        start(router_hbm, both_ref.at[1], sems.at[3]),
        start(logits_hbm, logits_ref, sems.at[0]),
        start(grads_hbm, grads_ref, sems.at[1]),
        start(x_hbm, x_ref, sems.at[4]),
    ]
    n, own, _ = parts_ref.shape
    loads[0].wait()
    loads[1].wait()
    copies = [start(both_ref, all_hbm.at[pl.ds(3 * j + 1, 2)], both_sems.at[j]) for j in range(n)]
    loads[2].wait()
    logits = logits_ref[...]
    weights = jnp.exp(logits - jnp.max(logits, axis=0, keepdims=True))
    probs = weights / jnp.sum(weights, axis=0, keepdims=True)
    probs_ref[...] = probs
    loads[3].wait()
    partial = dot(probs.astype(BF16), grads_ref[...], ((1,), (0,))).astype(BF16)
    for j in range(n):
        parts_ref[j] = partial[j * own : (j + 1) * own]
    copies += [start(parts_ref.at[j], all_hbm.at[3 * j], parts_sems.at[j]) for j in range(n)]
    for copy in copies + loads[4:]:
        copy.wait()


def forward_kernel(n_grp, *refs):
    x_refs = refs[:n_grp]
    w_gate_hbm, w_up_hbm, gate_ref, up_ref, w_gate_ref, w_up_ref, sems = refs[n_grp:]
    experts = gate_ref.shape[0]
    pairs = ((w_gate_hbm, w_gate_ref), (w_up_hbm, w_up_ref))
    copies = [[start(s.at[e], d.at[e], sems.at[i, e]) for i, (s, d) in enumerate(pairs)] for e in range(experts)]
    for e in range(experts):
        x = jnp.concatenate([r[e : e + 1] for r in x_refs], axis=0)
        copies[e][0].wait()
        gate_ref[e] = dot(x, w_gate_ref[e], ((1,), (1,)))
        copies[e][1].wait()
        up_ref[e] = dot(x, w_up_ref[e], ((1,), (1,)))


def load_kernel(so_ref, *refs):
    count = (len(refs) - 2) // 2
    pairs = tuple(zip(refs[:count], refs[count : 2 * count]))
    same_ref, sems = refs[2 * count :]
    copies = [start(s.at[e], d.at[e], sems.at[i, e]) for i, (s, d) in enumerate(pairs) for e in range(d.shape[0])]
    same_ref[...] = so_ref[...]
    for copy in copies:
        copy.wait()


def outer(left, right):
    n, rows = left.shape
    pad = -n % 8
    tall = left if pad == 0 else jnp.concatenate([left, jnp.zeros((pad, rows), F32)], axis=0)
    tall = tall.T
    total = tall[:, 0:1] * right[0:1]
    for s in range(1, n):
        total = total + tall[:, s : s + 1] * right[s : s + 1]
    return total.astype(BF16)


def put(value, buf_ref, out_hbm, sems, e, b):
    block = value.shape[0]
    span = pl.ds(b * block, block)
    buf_ref[e, span] = value
    start(buf_ref.at[e, span], out_hbm.at[e, span], sems.at[e, b])


def drain(out_hbm, buf_ref, sems):
    experts, blocks = sems.shape
    block = buf_ref.shape[1] // blocks

    @pl.loop(0, experts)
    def _(e):
        for b in range(blocks):
            span = pl.ds(b * block, block)
            pltpu.make_async_copy(buf_ref.at[e, span], out_hbm.at[e, span], sems.at[e, b]).wait()


def stack_rows(refs, into_ref):
    for e in range(into_ref.shape[0]):
        into_ref[e] = jnp.concatenate([r[e : e + 1] for r in refs], axis=0)


def middle_kernel(n_grp, block, *refs):
    so_refs, x_refs = refs[:n_grp], refs[n_grp : 2 * n_grp]
    gate_ref, up_ref, w_gate_hbm, w_up_hbm, w_down_ref = refs[2 * n_grp : 2 * n_grp + 5]
    partial_refs = refs[2 * n_grp + 5 : 3 * n_grp + 5]
    (up_grad_ref, grad_down_hbm, grad_gate_hbm, so_ref, x_ref, sum_ref, w_gate_ref, w_up_ref, down_buf, gate_buf,
     w_gate_sems, w_up_sems, down_sems, gate_sems) = refs[3 * n_grp + 5 :]
    experts, _, rows = gate_ref.shape
    blocks = rows // block

    def w_gate_copy(e):
        return pltpu.make_async_copy(w_gate_hbm.at[e], w_gate_ref.at[e], w_gate_sems.at[e])

    def w_up_copy(e):
        return pltpu.make_async_copy(w_up_hbm.at[e], w_up_ref.at[e], w_up_sems.at[e])

    for e in range(experts):
        w_gate_copy(e).start()
        w_up_copy(e).start()
    stack_rows(so_refs, so_ref)
    stack_rows(x_refs, x_ref)
    sum_ref[...] = jnp.zeros_like(sum_ref)

    def at(i):
        e, b = lax.div(i, blocks), lax.rem(i, blocks)
        return e, b, pl.ds(pl.multiple_of(b * block, block), block)

    def hidden_grad_at(i):
        e, b, span = at(i)
        return dot(so_ref[e], w_down_ref[e, span], ((1,), (1,)))

    def step(i, hidden_grad):
        e, b, span = at(i)

        @pl.when(b == 0)
        def _():
            w_gate_copy(e).wait()
            w_up_copy(e).wait()

        later = hidden_grad_at(jnp.minimum(i + 1, experts * blocks - 1))
        gate, up = gate_ref[e, :, span], up_ref[e, :, span]
        sig = 1.0 / (1.0 + jnp.exp(-gate))
        hidden = (gate * sig * up).astype(BF16)
        up_grad = (hidden_grad * gate * sig).astype(BF16)
        gate_grad = (hidden_grad * up * sig * (1.0 + gate * (1.0 - sig))).astype(BF16)
        up_grad_ref[e, :, span] = up_grad
        sum_ref[e] += dot(gate_grad, w_gate_ref[e, span], ((1,), (0,))) + dot(
            up_grad, w_up_ref[e, span], ((1,), (0,))
        )
        down_buf[e, span] = outer(hidden.astype(F32), so_ref[e].astype(F32))
        gate_buf[e, span] = outer(gate_grad.astype(F32), x_ref[e].astype(F32))
        start(down_buf.at[e, span], grad_down_hbm.at[e, span], down_sems.at[e, b])
        start(gate_buf.at[e, span], grad_gate_hbm.at[e, span], gate_sems.at[e, b])
        return later

    lax.fori_loop(0, experts * blocks, step, hidden_grad_at(0))
    for e in range(experts):
        for s, ref in enumerate(partial_refs):
            ref[e : e + 1] = sum_ref[e, s : s + 1].astype(ref.dtype)
    drain(grad_down_hbm, down_buf, down_sems)
    drain(grad_gate_hbm, gate_buf, gate_sems)


def last_kernel(n_grp, block, *refs):
    x_refs = refs[:n_grp]
    (up_grad_ref, probs_ref, grads_hbm, every_ref, partial_ref, grad_up_hbm, token_hbm, same_ref,
     x_ref, up_buf, grads_ref, token_ref, up_sems, sems) = refs[n_grp:]
    experts, _, rows = up_grad_ref.shape
    loaded = start(grads_hbm, grads_ref, sems.at[0])
    same_ref[...] = partial_ref[...]
    stack_rows(x_refs, x_ref)

    @pl.loop(0, experts)
    def _(e):
        x_wide = x_ref[e].astype(F32)
        for b in range(rows // block):
            up_grad = up_grad_ref[e, :, b * block : (b + 1) * block].astype(F32)
            put(outer(up_grad, x_wide), up_buf, grad_up_hbm, up_sems, e, b)

    probs = probs_ref[...]
    n = every_ref.shape[0] // 3
    outputs = jnp.concatenate([every_ref[3 * j + 1] for j in range(n)], axis=0)
    routers = jnp.concatenate([every_ref[3 * j + 2] for j in range(n)], axis=0)
    loaded.wait()
    weight_grad = dot(outputs, grads_ref[...], ((1,), (1,)))
    centre = jnp.sum(weight_grad * probs, axis=0, keepdims=True)
    logit_grad = (probs * (weight_grad - centre)).astype(BF16)
    token_ref[...] = dot(logit_grad, routers, ((0,), (0,))).astype(BF16)
    tokens = start(token_ref, token_hbm, sems.at[1])
    drain(grad_up_hbm, up_buf, up_sems)
    tokens.wait()


def shifted(x, size, k):
    return lax.ppermute(x, "grp", [((i + k) % size, i) for i in range(size)])


def per_device(n_seq, n_grp, out_grad, combine_logits, expert_out, slot_in, router, w_gate, w_up, w_down):
    grads = out_grad[0]
    own, width = router.shape
    rows = w_gate.shape[1]
    tokens = grads.shape[0]
    slots = n_seq * own
    block = min(256, rows)
    vec = (own, n_grp, rows)
    held = pltpu.VMEM((own, rows, width), BF16)
    big = shape((own, rows, width), BF16)
    buf = pltpu.VMEM((own, rows, width), BF16)
    few = pltpu.VMEM((own, n_grp, width), BF16)
    held_tokens = pltpu.VMEM((tokens, width), BF16)
    sems = SEMS((own, rows // block))
    probs, partial, x_own = call(
        soft_kernel, "soft",
        (shape((slots, tokens), F32), shape((3 * n_seq, own, width), BF16), shape((own, width), BF16)),
        (VMEM, HBM, VMEM),
        tuple(map(in_hbm, (combine_logits[0].T, grads, expert_out[0], router, slot_in[0]))), (HBM,) * 5,
        scratch=(pltpu.VMEM((slots, tokens), F32), held_tokens, pltpu.VMEM((2, own, width), BF16),
                 pltpu.VMEM((n_seq, own, width), BF16), SEMS((5,)), SEMS((n_seq,)), SEMS((n_seq,))),
    )
    every = lax.all_to_all(partial, "seq", split_axis=0, concat_axis=0, tiled=True)
    inputs = [x_own] + [shifted(x_own, n_grp, k) for k in range(1, n_grp)]
    gate, up = call(
        functools.partial(forward_kernel, n_grp), "forward", (shape(vec, F32), shape(vec, F32)), (VMEM, VMEM),
        (*inputs, in_hbm(w_gate), in_hbm(w_up)), (VMEM,) * n_grp + (HBM, HBM), scratch=(buf, buf, SEMS((2, own))),
        us=6, vmem=24 << 20,
    )
    slot_out = jnp.sum(every.reshape(n_seq, 3, own, width)[:, 0].astype(F32), axis=0).astype(BF16)
    others = [shifted(slot_out, n_grp, k) for k in range(1, n_grp)]
    w_down_v, same = call(
        load_kernel, "load", (held, shape((own, width), BF16)), (VMEM, VMEM),
        (slot_out, in_hbm(w_down)), (VMEM, HBM), scratch=(SEMS((1, own)),), us=3,
    )
    all_out = [same] + others
    *partials, up_grad, grad_down, grad_gate = call(
        functools.partial(middle_kernel, n_grp, block), "middle",
        (shape((own, width), F32),) + (shape((own, width), BF16),) * (n_grp - 1) + (shape(vec, BF16), big, big),
        (VMEM,) * (n_grp + 1) + (HBM, HBM),
        (*all_out, *inputs, gate, up, in_hbm(w_gate), in_hbm(w_up), w_down_v),
        (VMEM,) * (2 * n_grp + 2) + (HBM, HBM, VMEM),
        scratch=(few, few, pltpu.VMEM((own, n_grp, width), F32), buf, buf, buf, buf,
                 SEMS((own,)), SEMS((own,)), sems, sems),
        us=8, vmem=40 << 20,
    )
    with jax.named_scope("back"):
        back = [shifted(partials[k], n_grp, n_grp - k) for k in range(1, n_grp)]
    with jax.named_scope("ending"):
        grad_up, token_grad, slot_grad = call(
            functools.partial(last_kernel, n_grp, block), "last",
            (big, shape((tokens, width), BF16), shape((own, width), F32)), (HBM, HBM, VMEM),
            (*inputs, up_grad, probs, in_hbm(grads), every, partials[0]),
            (VMEM,) * (n_grp + 2) + (HBM, VMEM, VMEM),
            scratch=(few, buf, held_tokens, held_tokens, sems, SEMS((2,))), us=5, vmem=24 << 20,
        )
    for part in back:
        slot_grad = slot_grad + part.astype(F32)
    return token_grad[None], slot_grad[None], grad_gate, grad_up, grad_down


def solution(mesh):
    def body(*args):
        return per_device(mesh.shape["seq"], mesh.shape["grp"], *args)

    tokens, weights = P("grp", "seq", None), P("seq", "grp", None)
    return jax.shard_map(
        body,
        mesh=mesh,
        in_specs=(tokens, tokens, tokens, tokens, P("seq", None), weights, weights, weights),
        out_specs=(tokens, tokens, weights, weights, weights),
        check_vma=False,
    )
```

time: 63.6 us -> 47.7 us (0.75)
  matrix products: 39.3 us -> 0 us
  Pallas kernels: 0 us -> 31.3 us
  starting transfers between devices: 16.6 us -> 11.1 us
  waiting for transfers between devices: 0.79 us -> 3.6 us
  other arithmetic: 3.15 us -> 0.68 us
  local copies, waits for them, and re-layouts: 2.44 us -> 0 us
    dot_general x11 -> x0, matrix products: 39.3 us -> none  [the longest x1 5.82 us: slot_backward(): jnp.einsum('gef,ged->efd', hidden, out_grads, preferred_element_type=F32)]
    pallas_call x0 -> x5, Pallas kernels: none -> 31.3 us  [call(): pl.pallas_call(body, name=name, out_shape=outs, in_specs=in_specs, out_sp...]
    all_to_all x2 -> x1, starting transfers between devices: 11.3 us -> 7.4 us  [per_device(): lax.all_to_all(partial, 'seq', split_axis=0, concat_axis=0, tiled=True)]
    ppermute x3, waiting for transfers between devices: 0.01 us -> 2.14 us  [shifted(): return lax.ppermute(x, 'grp', [((i + k) % size, i) for i in range(size)])]
    ppermute x3, starting transfers between devices: 5.21 us -> 3.73 us  [shifted(): return lax.ppermute(x, 'grp', [((i + k) % size, i) for i in range(size)])]
    reduce_sum x2 -> x1, other arithmetic: 0.95 us -> 0.07 us  [per_device(): jnp.sum(every.reshape(n_seq, 3, own, width)[:, 0].astype(F32), axis=0)]
    reduce_max x1 -> x0, other arithmetic: 0.86 us -> none  [per_device(): probs = jax.nn.softmax(combine_logits[0], axis=-1)]
    reshape x3 -> x0, local copies, waits for them, and re-layouts: 0.78 us -> none  [the longest x1 0.71 us: per_device(): partial.astype(BF16).reshape(n_seq, own, width)]
  transfers between devices with their start and end apart: 5 -> 4, of which waited for: 1 -> 2; matrix products, arithmetic and copies ran while one was open for 68% -> 0% of each run, Pallas kernels for 0% -> 33%
where the time goes in v2:
time: 47.7 us; the launch traced here: 47.5 us
  Pallas kernels  31.3 us (66%)
  starting transfers between devices  11.1 us (23%)
  waiting for transfers between devices  3.6 us (8%)
  between operations  0.7 us (1%)
  other arithmetic  0.68 us (1%)
    pallas_call x5, Pallas kernels, call(): pl.pallas_call(body, name=name, out_shape=outs, in_specs=in_specs, out_sp...  31.3 us
    all_to_all x1, starting transfers between devices, per_device(): lax.all_to_all(partial, 'seq', split_axis=0, concat_axis=0, tiled=True)  7.4 us
    ppermute x3, starting transfers between devices, shifted(): return lax.ppermute(x, 'grp', [((i + k) % size, i) for i in range(size)])  3.73 us
    ppermute x3, waiting for transfers between devices, shifted(): return lax.ppermute(x, 'grp', [((i + k) % size, i) for i in range(size)])  2.14 us
    all_to_all x1, waiting for transfers between devices, per_device(): lax.all_to_all(partial, 'seq', split_axis=0, concat_axis=0, tiled=True)  1.47 us
  transfers between devices with their start and end apart: 4, of which 2 were waited for; matrix products, arithmetic and copies ran while one was open for 0% of the time, Pallas kernels for 33%

profile of v2, /device:TPU:0, one launch (start us, length us, event | category | flops | bytes accessed | tf_op | source)
XLA Modules:
  0.0 47.5 jit_solution(4304853465109242759)
XLA Ops:
  0.6 2.3 %soft.1 = (f32[64,216]{1,0:T(8,128)S(1)}, bf16[48,4,1024]{2,1,0:T(4,128)(2,1)}, bf16[4,1024]{1,0:T(4,128)(2,1)S(1)}) custom-call(f32[64,216]{1,0:T(8,128)} %bitcast.13, bf16[216,1024]{1,0:T(8,128)(2,1)} %bitcast.11, bf16[4,1024]{1,0:T(4,128)(2,1)} %bitcast.14, bf16[4,1024]{1,0:T(4,128)(2,1)} %router_hbm.1, bf16[4,1024]{1,0:T(4,128)(2,1)} %bitcast.15), custom_call_target="tpu_custom_call" | custom-call | flops 800000000 | bytes 3000000 | tf_op jit(solution)/shard_map/soft/pallas_call | solution.py:36
  2.9 7.4 %all-to-all-start = ((bf16[48,4,1024]{2,1,0:T(4,128)(2,1)}), bf16[48,4,1024]{2,1,0:T(4,128)(2,1)S(1)}, u32[]{:S(2)}, u32[]{:S(2)}) async-start(bf16[48,4,1024]{2,1,0:T(4,128)(2,1)} %get-tuple-element.21), calls=%async_computation | async-start | bytes 786432 | tf_op jit(solution)/shard_map/all_to_all | solution.py:251
  10.3 1.6 %collective-permute-start = (bf16[4,1024]{1,0:T(4,128)(2,1)S(1)}, bf16[4,1024]{1,0:T(4,128)(2,1)S(1)}, u32[]{:S(2)}, u32[]{:S(2)}) collective-permute-start(bf16[4,1024]{1,0:T(4,128)(2,1)S(1)} %get-tuple-element.20.refs_0_.refs_2_), channel_id=1, source_target_pairs={{1,0},{0,1},{3,2},{2,3},{5,4},{4,5},{7,6},{6,7},{9,8},{8,9},{11,10... | collective-permute-start | bytes 24584 | tf_op jit(solution)/shard_map/ppermute | solution.py:226
  11.9 2.1 %collective-permute-done.refs_1_.refs_3_ = bf16[4,1024]{1,0:T(4,128)(2,1)S(1)} collective-permute-done((bf16[4,1024]{1,0:T(4,128)(2,1)S(1)}, bf16[4,1024]{1,0:T(4,128)(2,1)S(1)}, u32[]{:S(2)}, u32[]{:S(2)}) %collective-permute-start) | collective-permute-done | bytes 8224 | tf_op jit(solution)/shard_map/ppermute | solution.py:226
  14.0 7.0 %forward.1 = (f32[4,2,1024]{2,1,0:T(2,128)S(1)}, f32[4,2,1024]{2,1,0:T(2,128)S(1)}) custom-call(bf16[4,1024]{1,0:T(4,128)(2,1)S(1)} %get-tuple-element.20.refs_0_.refs_2_, bf16[4,1024]{1,0:T(4,128)(2,1)S(1)} %collective-permute-done.refs_1_.refs_3_, bf16[4,1024,1024]{2,1,0:T(8,128)(2,1)} %refs_6_.1, bf16[4,1024,1024]{2,1,0:T(8,128)(2,1)} %refs_7_.1), custom_call_target="tpu_custom_call" | custom-call | flops 4800000000 | bytes 18000000 | tf_op jit(solution)/shard_map/forward/pallas_call | solution.py:36
  21.0 1.5 %all-to-all-done.refs_5_ = bf16[48,4,1024]{2,1,0:T(4,128)(2,1)S(1)} async-done(((bf16[48,4,1024]{2,1,0:T(4,128)(2,1)}), bf16[48,4,1024]{2,1,0:T(4,128)(2,1)S(1)}, u32[]{:S(2)}, u32[]{:S(2)}) %all-to-all-start) | async-done | bytes 393248 | tf_op jit(solution)/shard_map/all_to_all | solution.py:251
  22.5 0.1 slice_reduce_fusion.so_ref
  22.6 1.6 %collective-permute-start.1 = (bf16[4,1024]{1,0:T(4,128)(2,1)S(1)}, bf16[4,1024]{1,0:T(4,128)(2,1)S(1)}, u32[]{:S(2)}, u32[]{:S(2)}) collective-permute-start(bf16[4,1024]{1,0:T(4,128)(2,1)S(1)} %slice_reduce_fusion.so_ref), channel_id=1, source_target_pairs={{1,0},{0,1},{3,2},{2,3},{5,4},{4,5},{7,6},{6,7},{9,8},{8,9},{11,10... | collective-permute-start | bytes 24584 | tf_op jit(solution)/shard_map/ppermute | solution.py:226
  24.1 3.5 %load.1 = (bf16[4,1024,1024]{2,1,0:T(8,128)(2,1)S(1)}, bf16[4,1024]{1,0:T(4,128)(2,1)S(1)}) custom-call(bf16[4,1024]{1,0:T(4,128)(2,1)S(1)} %slice_reduce_fusion.so_ref, bf16[4,1024,1024]{2,1,0:T(8,128)(2,1)} %refs_0_.1), custom_call_target="tpu_custom_call" | custom-call | flops 2400000000 | bytes 9000000 | tf_op jit(solution)/shard_map/load/pallas_call | solution.py:36
  27.6 0.0 collective-permute-done.1.refs_1_
  27.7 13.5 %middle.1 = (f32[4,1024]{1,0:T(4,128)S(1)}, bf16[4,1024]{1,0:T(4,128)(2,1)S(1)}, bf16[4,2,1024]{2,1,0:T(2,128)(2,1)S(1)}, bf16[4,1024,1024]{2,1,0:T(8,128)(2,1)}, bf16[4,1024,1024]{2,1,0:T(8,128)(2,1)}) custom-call(bf16[4,1024]{1,0:T(4,128)(2,1)S(1)} %get-tuple-element.22.refs_0_, bf16[4,1024]{1,0:T(4,128)(2,1)S(1)} %collective-permute-done.1.refs_1_, ...), custom_call_target="tpu_custom_call" | custom-call | flops 6400000000 | bytes 24000000 | tf_op jit(solution)/shard_map/middle/pallas_call | solution.py:36
  41.1 0.6 %collective-permute-start.2 = (bf16[4,1024]{1,0:T(4,128)(2,1)S(1)}, bf16[4,1024]{1,0:T(4,128)(2,1)S(1)}, u32[]{:S(2)}, u32[]{:S(2)}) collective-permute-start(bf16[4,1024]{1,0:T(4,128)(2,1)S(1)} %get-tuple-element.31), channel_id=1, source_target_pairs={{1,0},{0,1},{3,2},{2,3},{5,4},{4,5},{7,6},{6,7},{9,8},{8,9},{11,10... | collective-permute-start | bytes 24584 | tf_op jit(solution)/shard_map/back/ppermute | solution.py:226
  41.7 5.1 %last.1 = (bf16[4,1024,1024]{2,1,0:T(8,128)(2,1)}, bf16[216,1024]{1,0:T(8,128)(2,1)}, f32[4,1024]{1,0:T(4,128)S(1)}) custom-call(bf16[4,1024]{1,0:T(4,128)(2,1)S(1)} %get-tuple-element.20.refs_0_.refs_2_, bf16[4,1024]{1,0:T(4,128)(2,1)S(1)} %collective-permute-done.refs_1_.refs_3_, bf16[4,2,1024]{2,1,0:T(2,128)(2,1)S(1)} %get-tuple-element.26.refs_2_, ...), custom_call_target="tpu_custom_call" | custom-call | flops 4000000000 | bytes 15000000 | tf_op jit(solution)/shard_map/ending/last/pallas_call | solution.py:36
  46.8 0.0 collective-permute-done.2
  46.8 0.6 %add_bitcast_fusion = f32[1,4,1024]{2,1,0:T(4,128)} fusion(f32[4,1024]{1,0:T(4,128)S(1)} %get-tuple-element.30, bf16[4,1024]{1,0:T(4,128)(2,1)S(1)} %collective-permute-done.2), kind=kLoop, calls=%fused_computation.1 | loop fusion | flops 8192 | bytes 40960 | tf_op jit(solution)/shard_map/broadcast_in_dim | solution.py:287
Async XLA Ops:
  2.9 19.6 %all-to-all-start = ((bf16[48,4,1024]{2,1,0:T(4,128)(2,1)}), bf16[48,4,1024]{2,1,0:T(4,128)(2,1)S(1)}, u32[]{:S(2)}, u32[]{:S(2)}) async-start(bf16[48,4,1024]{2,1,0:T(4,128)(2,1)} %get-tuple-element.21), calls=%async_computation | async-start | bytes 786432 | tf_op jit(solution)/shard_map/all_to_all | solution.py:251
  10.3 3.7 %collective-permute-start = (bf16[4,1024]{1,0:T(4,128)(2,1)S(1)}, bf16[4,1024]{1,0:T(4,128)(2,1)S(1)}, u32[]{:S(2)}, u32[]{:S(2)}) collective-permute-start(bf16[4,1024]{1,0:T(4,128)(2,1)S(1)} %get-tuple-element.20.refs_0_.refs_2_), channel_id=1, source_target_pairs={{1,0},{0,1},{3,2},{2,3},{5,4},{4,5},{7,6},{6,7},{9,8},{8,9},{11,10... | collective-permute-start | bytes 24584 | tf_op jit(solution)/shard_map/ppermute | solution.py:226
  22.6 5.1 %collective-permute-start.1 = (bf16[4,1024]{1,0:T(4,128)(2,1)S(1)}, bf16[4,1024]{1,0:T(4,128)(2,1)S(1)}, u32[]{:S(2)}, u32[]{:S(2)}) collective-permute-start(bf16[4,1024]{1,0:T(4,128)(2,1)S(1)} %slice_reduce_fusion.so_ref), channel_id=1, source_target_pairs={{1,0},{0,1},{3,2},{2,3},{5,4},{4,5},{7,6},{6,7},{9,8},{8,9},{11,10... | collective-permute-start | bytes 24584 | tf_op jit(solution)/shard_map/ppermute | solution.py:226
  41.1 5.7 %collective-permute-start.2 = (bf16[4,1024]{1,0:T(4,128)(2,1)S(1)}, bf16[4,1024]{1,0:T(4,128)(2,1)S(1)}, u32[]{:S(2)}, u32[]{:S(2)}) collective-permute-start(bf16[4,1024]{1,0:T(4,128)(2,1)S(1)} %get-tuple-element.31), channel_id=1, source_target_pairs={{1,0},{0,1},{3,2},{2,3},{5,4},{4,5},{7,6},{6,7},{9,8},{8,9},{11,10... | collective-permute-start | bytes 24584 | tf_op jit(solution)/shard_map/back/ppermute | solution.py:226

commit v3 on v2

--- a/solution.py
+++ b/solution.py
@@ -86,32 +86,38 @@
         up_ref[e] = dot(x, w_up_ref[e], ((1,), (1,)))
 
 
-def load_kernel(so_ref, *refs):
-    count = (len(refs) - 2) // 2
-    pairs = tuple(zip(refs[:count], refs[count : 2 * count]))
-    same_ref, sems = refs[2 * count :]
-    copies = [start(s.at[e], d.at[e], sems.at[i, e]) for i, (s, d) in enumerate(pairs) for e in range(d.shape[0])]
-    same_ref[...] = so_ref[...]
-    for copy in copies:
-        copy.wait()
-
-
-def outer(left, right):
+def sum_kernel(every_ref, after_ref, out_ref):
+    del after_ref
+    total = every_ref[0].astype(F32)
+    for j in range(3, every_ref.shape[0], 3):
+        total = total + every_ref[j].astype(F32)
+    out_ref[...] = total.astype(BF16)
+
+
+def pause_kernel(x_ref, same_ref):
+    same_ref[...] = x_ref[...]
+
+
+def outer_into(left, right, buf_ref, e, block=256):
     n, rows = left.shape
     pad = -n % 8
     tall = left if pad == 0 else jnp.concatenate([left, jnp.zeros((pad, rows), F32)], axis=0)
-    tall = tall.T
-    total = tall[:, 0:1] * right[0:1]
-    for s in range(1, n):
-        total = total + tall[:, s : s + 1] * right[s : s + 1]
-    return total.astype(BF16)
-
-
-def put(value, buf_ref, out_hbm, sems, e, b):
-    block = value.shape[0]
-    span = pl.ds(b * block, block)
-    buf_ref[e, span] = value
-    start(buf_ref.at[e, span], out_hbm.at[e, span], sems.at[e, b])
+    tall, right = tall.T.astype(BF16), right.astype(BF16)
+    block = min(block, rows)
+    for b in range(0, rows, block):
+        part = tall[b : b + block]
+        total = part[:, 0:1] * right[0:1]
+        for s in range(1, n):
+            total = total + part[:, s : s + 1] * right[s : s + 1]
+        buf_ref[e, pl.ds(b, block)] = total
+
+
+def send(buf_ref, out_hbm, sems, e):
+    blocks = sems.shape[1]
+    block = buf_ref.shape[1] // blocks
+    for b in range(blocks):
+        span = pl.ds(b * block, block)
+        start(buf_ref.at[e, span], out_hbm.at[e, span], sems.at[e, b])
 
 
 def drain(out_hbm, buf_ref, sems):
@@ -130,61 +136,44 @@
         into_ref[e] = jnp.concatenate([r[e : e + 1] for r in refs], axis=0)
 
 
-def middle_kernel(n_grp, block, *refs):
+def middle_kernel(n_grp, *refs):
     so_refs, x_refs = refs[:n_grp], refs[n_grp : 2 * n_grp]
-    gate_ref, up_ref, w_gate_hbm, w_up_hbm, w_down_ref = refs[2 * n_grp : 2 * n_grp + 5]
+    gate_ref, up_ref, w_gate_hbm, w_up_ref, w_down_ref = refs[2 * n_grp : 2 * n_grp + 5]
     partial_refs = refs[2 * n_grp + 5 : 3 * n_grp + 5]
-    (up_grad_ref, grad_down_hbm, grad_gate_hbm, so_ref, x_ref, sum_ref, w_gate_ref, w_up_ref, down_buf, gate_buf,
-     w_gate_sems, w_up_sems, down_sems, gate_sems) = refs[3 * n_grp + 5 :]
-    experts, _, rows = gate_ref.shape
-    blocks = rows // block
+    (up_grad_ref, grad_down_hbm, grad_gate_hbm, so_ref, x_ref, sum_ref, w_gate_ref, down_buf, gate_buf,
+     w_gate_sems, down_sems, gate_sems) = refs[3 * n_grp + 5 :]
+    experts = gate_ref.shape[0]
 
     def w_gate_copy(e):
         return pltpu.make_async_copy(w_gate_hbm.at[e], w_gate_ref.at[e], w_gate_sems.at[e])
 
-    def w_up_copy(e):
-        return pltpu.make_async_copy(w_up_hbm.at[e], w_up_ref.at[e], w_up_sems.at[e])
-
     for e in range(experts):
         w_gate_copy(e).start()
-        w_up_copy(e).start()
     stack_rows(so_refs, so_ref)
     stack_rows(x_refs, x_ref)
-    sum_ref[...] = jnp.zeros_like(sum_ref)
-
-    def at(i):
-        e, b = lax.div(i, blocks), lax.rem(i, blocks)
-        return e, b, pl.ds(pl.multiple_of(b * block, block), block)
-
-    def hidden_grad_at(i):
-        e, b, span = at(i)
-        return dot(so_ref[e], w_down_ref[e, span], ((1,), (1,)))
-
-    def step(i, hidden_grad):
-        e, b, span = at(i)
-
-        @pl.when(b == 0)
-        def _():
-            w_gate_copy(e).wait()
-            w_up_copy(e).wait()
-
-        later = hidden_grad_at(jnp.minimum(i + 1, experts * blocks - 1))
-        gate, up = gate_ref[e, :, span], up_ref[e, :, span]
+
+    def hidden_grad_of(e):
+        return dot(so_ref[e], w_down_ref[e], ((1,), (1,)))
+
+    def step(e, hidden_grad):
+        w_gate_copy(e).wait()
+        gate, up = gate_ref[e], up_ref[e]
         sig = 1.0 / (1.0 + jnp.exp(-gate))
         hidden = (gate * sig * up).astype(BF16)
         up_grad = (hidden_grad * gate * sig).astype(BF16)
         gate_grad = (hidden_grad * up * sig * (1.0 + gate * (1.0 - sig))).astype(BF16)
-        up_grad_ref[e, :, span] = up_grad
-        sum_ref[e] += dot(gate_grad, w_gate_ref[e, span], ((1,), (0,))) + dot(
-            up_grad, w_up_ref[e, span], ((1,), (0,))
-        )
-        down_buf[e, span] = outer(hidden.astype(F32), so_ref[e].astype(F32))
-        gate_buf[e, span] = outer(gate_grad.astype(F32), x_ref[e].astype(F32))
-        start(down_buf.at[e, span], grad_down_hbm.at[e, span], down_sems.at[e, b])
-        start(gate_buf.at[e, span], grad_gate_hbm.at[e, span], gate_sems.at[e, b])
+        up_grad_ref[e] = up_grad
+        later = hidden_grad_of(min(e + 1, experts - 1))
+        sum_ref[e] = dot(gate_grad, w_gate_ref[e], ((1,), (0,))) + dot(up_grad, w_up_ref[e], ((1,), (0,)))
+        outer_into(hidden.astype(F32), so_ref[e].astype(F32), down_buf, e)
+        outer_into(gate_grad.astype(F32), x_ref[e].astype(F32), gate_buf, e)
+        send(down_buf, grad_down_hbm, down_sems, e)
+        send(gate_buf, grad_gate_hbm, gate_sems, e)
         return later
 
-    lax.fori_loop(0, experts * blocks, step, hidden_grad_at(0))
+    later = hidden_grad_of(0)
+    for e in range(experts):
+        later = step(e, later)
     for e in range(experts):
         for s, ref in enumerate(partial_refs):
             ref[e : e + 1] = sum_ref[e, s : s + 1].astype(ref.dtype)
@@ -192,21 +181,19 @@
     drain(grad_gate_hbm, gate_buf, gate_sems)
 
 
-def last_kernel(n_grp, block, *refs):
+def last_kernel(n_grp, *refs):
     x_refs = refs[:n_grp]
     (up_grad_ref, probs_ref, grads_hbm, every_ref, partial_ref, grad_up_hbm, token_hbm, same_ref,
      x_ref, up_buf, grads_ref, token_ref, up_sems, sems) = refs[n_grp:]
-    experts, _, rows = up_grad_ref.shape
+    experts = up_grad_ref.shape[0]
     loaded = start(grads_hbm, grads_ref, sems.at[0])
     same_ref[...] = partial_ref[...]
     stack_rows(x_refs, x_ref)
 
     @pl.loop(0, experts)
     def _(e):
-        x_wide = x_ref[e].astype(F32)
-        for b in range(rows // block):
-            up_grad = up_grad_ref[e, :, b * block : (b + 1) * block].astype(F32)
-            put(outer(up_grad, x_wide), up_buf, grad_up_hbm, up_sems, e, b)
+        outer_into(up_grad_ref[e].astype(F32), x_ref[e].astype(F32), up_buf, e)
+        send(up_buf, grad_up_hbm, up_sems, e)
 
     probs = probs_ref[...]
     n = every_ref.shape[0] // 3
@@ -255,28 +242,24 @@
         (*inputs, in_hbm(w_gate), in_hbm(w_up)), (VMEM,) * n_grp + (HBM, HBM), scratch=(buf, buf, SEMS((2, own))),
         us=6, vmem=24 << 20,
     )
-    slot_out = jnp.sum(every.reshape(n_seq, 3, own, width)[:, 0].astype(F32), axis=0).astype(BF16)
-    others = [shifted(slot_out, n_grp, k) for k in range(1, n_grp)]
-    w_down_v, same = call(
-        load_kernel, "load", (held, shape((own, width), BF16)), (VMEM, VMEM),
-        (slot_out, in_hbm(w_down)), (VMEM, HBM), scratch=(SEMS((1, own)),), us=3,
-    )
-    all_out = [same] + others
+    slot_out = call(sum_kernel, "sum", shape((own, width), BF16), VMEM, (every, gate), (VMEM, VMEM), us=20)
+    same = call(pause_kernel, "pause", shape((own, width), BF16), VMEM, (slot_out,), (VMEM,), us=20)
+    all_out = [same] + [shifted(slot_out, n_grp, k) for k in range(1, n_grp)]
     *partials, up_grad, grad_down, grad_gate = call(
-        functools.partial(middle_kernel, n_grp, block), "middle",
+        functools.partial(middle_kernel, n_grp), "middle",
         (shape((own, width), F32),) + (shape((own, width), BF16),) * (n_grp - 1) + (shape(vec, BF16), big, big),
         (VMEM,) * (n_grp + 1) + (HBM, HBM),
-        (*all_out, *inputs, gate, up, in_hbm(w_gate), in_hbm(w_up), w_down_v),
-        (VMEM,) * (2 * n_grp + 2) + (HBM, HBM, VMEM),
-        scratch=(few, few, pltpu.VMEM((own, n_grp, width), F32), buf, buf, buf, buf,
-                 SEMS((own,)), SEMS((own,)), sems, sems),
-        us=8, vmem=40 << 20,
+        (*all_out, *inputs, gate, up, in_hbm(w_gate), w_up, w_down),
+        (VMEM,) * (2 * n_grp + 2) + (HBM, VMEM, VMEM),
+        scratch=(few, few, pltpu.VMEM((own, n_grp, width), F32), buf, buf, buf,
+                 SEMS((own,)), sems, sems),
+        us=8, vmem=32 << 20,
     )
     with jax.named_scope("back"):
         back = [shifted(partials[k], n_grp, n_grp - k) for k in range(1, n_grp)]
     with jax.named_scope("ending"):
         grad_up, token_grad, slot_grad = call(
-            functools.partial(last_kernel, n_grp, block), "last",
+            functools.partial(last_kernel, n_grp), "last",
             (big, shape((tokens, width), BF16), shape((own, width), F32)), (HBM, HBM, VMEM),
             (*inputs, up_grad, probs, in_hbm(grads), every, partials[0]),
             (VMEM,) * (n_grp + 2) + (HBM, VMEM, VMEM),

time: 47.7 us -> 44.6 us (0.935)
  Pallas kernels: 31.3 us -> 23 us
  waiting for transfers between devices: 3.6 us -> 5.73 us
  local copies, waits for them, and re-layouts: 0 us -> 2.1 us
  starting transfers between devices: 11.1 us -> 12.2 us
    pallas_call x5 -> x6, Pallas kernels: 31.3 us -> 23 us  [call(): pl.pallas_call(body, name=name, out_shape=outs, in_specs=in_specs, out_sp...]
    ppermute x3, waiting for transfers between devices: 2.14 us -> 4.26 us  [shifted(): return lax.ppermute(x, 'grp', [((i + k) % size, i) for i in range(size)])]
    unnamed x0 -> x8, local copies, waits for them, and re-layouts: none -> 2.1 us
    ppermute x3, starting transfers between devices: 3.73 us -> 4.75 us  [shifted(): return lax.ppermute(x, 'grp', [((i + k) % size, i) for i in range(size)])]
  transfers between devices with their start and end apart: 4 -> 4, of which waited for: 2 -> 3; matrix products, arithmetic and copies ran while one was open for 0% -> 0% of each run, Pallas kernels for 33% -> 25%
where the time goes in v3:
time: 44.6 us; the launch traced here: 44.3 us
  Pallas kernels  23 us (52%)
  starting transfers between devices  12.2 us (27%)
  waiting for transfers between devices  5.73 us (13%)
  local copies, waits for them, and re-layouts  2.1 us (5%)
  between operations  0.7 us (2%)
  other arithmetic  0.61 us (1%)
    pallas_call x6, Pallas kernels, call(): pl.pallas_call(body, name=name, out_shape=outs, in_specs=in_specs, out_sp...  23 us
    all_to_all x1, starting transfers between devices, per_device(): lax.all_to_all(partial, 'seq', split_axis=0, concat_axis=0, tiled=True)  7.4 us
    ppermute x3, starting transfers between devices, shifted(): return lax.ppermute(x, 'grp', [((i + k) % size, i) for i in range(size)])  4.75 us
    ppermute x3, waiting for transfers between devices, shifted(): return lax.ppermute(x, 'grp', [((i + k) % size, i) for i in range(size)])  4.26 us
    unnamed x8, local copies, waits for them, and re-layouts  2.1 us
    all_to_all x1, waiting for transfers between devices, per_device(): lax.all_to_all(partial, 'seq', split_axis=0, concat_axis=0, tiled=True)  1.47 us
  transfers between devices with their start and end apart: 4, of which 3 were waited for; matrix products, arithmetic and copies ran while one was open for 0% of the time, Pallas kernels for 25%

profile of v3, /device:TPU:0, one launch (start us, length us, event | category | flops | bytes accessed | tf_op | source)
XLA Modules:
  0.0 44.3 jit_solution(9498751636636963869)
XLA Ops:
  0.6 2.3 %soft.1 = (f32[64,216]{1,0:T(8,128)S(1)}, bf16[48,4,1024]{2,1,0:T(4,128)(2,1)}, bf16[4,1024]{1,0:T(4,128)(2,1)S(1)}) custom-call(f32[64,216]{1,0:T(8,128)} %bitcast.15, bf16[216,1024]{1,0:T(8,128)(2,1)} %bitcast.13, bf16[4,1024]{1,0:T(4,128)(2,1)} %bitcast.16, bf16[4,1024]{1,0:T(4,128)(2,1)} %router_hbm.1, bf16[4,1024]{1,0:T(4,128)(2,1)} %bitcast.17), custom_call_target="tpu_custom_call" | custom-call | flops 800000000 | bytes 3000000 | tf_op jit(solution)/shard_map/soft/pallas_call | solution.py:36
  2.9 7.4 %all-to-all-start = ((bf16[48,4,1024]{2,1,0:T(4,128)(2,1)}), bf16[48,4,1024]{2,1,0:T(4,128)(2,1)S(1)}, u32[]{:S(2)}, u32[]{:S(2)}) async-start(bf16[48,4,1024]{2,1,0:T(4,128)(2,1)} %get-tuple-element.19), calls=%async_computation | async-start | bytes 786432 | tf_op jit(solution)/shard_map/all_to_all | solution.py:238
  10.3 1.6 %collective-permute-start = (bf16[4,1024]{1,0:T(4,128)(2,1)S(1)}, bf16[4,1024]{1,0:T(4,128)(2,1)S(1)}, u32[]{:S(2)}, u32[]{:S(2)}) collective-permute-start(bf16[4,1024]{1,0:T(4,128)(2,1)S(1)} %get-tuple-element.18.refs_0_.refs_2_), channel_id=1, source_target_pairs={{1,0},{0,1},{3,2},{2,3},{5,4},{4,5},{7,6},{6,7},{9,8},{8,9},{11,10... | collective-permute-start | bytes 24584 | tf_op jit(solution)/shard_map/ppermute | solution.py:213
  11.9 2.1 %collective-permute-done.refs_1_.refs_3_ = bf16[4,1024]{1,0:T(4,128)(2,1)S(1)} collective-permute-done((bf16[4,1024]{1,0:T(4,128)(2,1)S(1)}, bf16[4,1024]{1,0:T(4,128)(2,1)S(1)}, u32[]{:S(2)}, u32[]{:S(2)}) %collective-permute-start) | collective-permute-done | bytes 8224 | tf_op jit(solution)/shard_map/ppermute | solution.py:213
  14.0 7.0 %forward.1 = (f32[4,2,1024]{2,1,0:T(2,128)S(1)}, f32[4,2,1024]{2,1,0:T(2,128)S(1)}) custom-call(bf16[4,1024]{1,0:T(4,128)(2,1)S(1)} %get-tuple-element.18.refs_0_.refs_2_, bf16[4,1024]{1,0:T(4,128)(2,1)S(1)} %collective-permute-done.refs_1_.refs_3_, bf16[4,1024,1024]{2,1,0:T(8,128)(2,1)} %refs_6_.1, bf16[4,1024,1024]{2,1,0:T(8,128)(2,1)} %refs_7_.1), custom_call_target="tpu_custom_call" | custom-call | flops 4800000000 | bytes 18000000 | tf_op jit(solution)/shard_map/forward/pallas_call | solution.py:36
  21.0 1.5 %all-to-all-done.every_ref.refs_5_ = bf16[48,4,1024]{2,1,0:T(4,128)(2,1)S(1)} async-done(((bf16[48,4,1024]{2,1,0:T(4,128)(2,1)}), bf16[48,4,1024]{2,1,0:T(4,128)(2,1)S(1)}, u32[]{:S(2)}, u32[]{:S(2)}) %all-to-all-start) | async-done | bytes 393248 | tf_op jit(solution)/shard_map/all_to_all | solution.py:238
  22.5 0.0 slice-start
  22.5 0.0 slice-start.2
  22.5 0.0 slice-start.1
  22.5 0.0 slice-start.3
  22.5 1.6 %collective-permute-start.1 = (bf16[4,1024]{1,0:T(4,128)(2,1)S(1)}, bf16[4,1024]{1,0:T(4,128)(2,1)S(1)}, u32[]{:S(2)}, u32[]{:S(2)}) collective-permute-start(bf16[4,1024]{1,0:T(4,128)(2,1)S(1)} %sum.1.x_ref), channel_id=1, source_target_pairs={{1,0},{0,1},{3,2},{2,3},{5,4},{4,5},{7,6},{6,7},{9,8},{8,9},{11,10... | collective-permute-start | bytes 24584 | tf_op jit(solution)/shard_map/ppermute | solution.py:213
  24.1 2.1 %collective-permute-done.1.refs_1_ = bf16[4,1024]{1,0:T(4,128)(2,1)S(1)} collective-permute-done((bf16[4,1024]{1,0:T(4,128)(2,1)S(1)}, bf16[4,1024]{1,0:T(4,128)(2,1)S(1)}, u32[]{:S(2)}, u32[]{:S(2)}) %collective-permute-start.1) | collective-permute-done | bytes 8224 | tf_op jit(solution)/shard_map/ppermute | solution.py:213
  26.3 0.0 slice-done
  26.3 0.0 slice-done.2
  26.3 0.9 %slice-done.1 = s8[4194304]{0:T(1024)(128)(4,1)S(1)} async-done(((s8[8388608]{0:T(1024)(128)(4,1)}), s8[4194304]{0:T(1024)(128)(4,1)S(1)}, s32[]{:S(2)}) %slice-start.1) | async-done | bytes 4194328
  27.2 1.2 %slice-done.3 = s8[4194304]{0:T(1024)(128)(4,1)S(1)} async-done(((s8[8388608]{0:T(1024)(128)(4,1)}), s8[4194304]{0:T(1024)(128)(4,1)S(1)}, s32[]{:S(2)}) %slice-start.3) | async-done | bytes 4194328
  28.4 9.6 %middle.1 = (f32[4,1024]{1,0:T(4,128)S(1)}, bf16[4,1024]{1,0:T(4,128)(2,1)S(1)}, bf16[4,2,1024]{2,1,0:T(2,128)(2,1)S(1)}, bf16[4,1024,1024]{2,1,0:T(8,128)(2,1)}, bf16[4,1024,1024]{2,1,0:T(8,128)(2,1)}) custom-call(bf16[4,1024]{1,0:T(4,128)(2,1)S(1)} %pause.1.refs_0_, bf16[4,1024]{1,0:T(4,128)(2,1)S(1)} %collective-permute-done.1.refs_1_, ...), custom_call_target="tpu_custom_call" | custom-call | flops 6400000000 | bytes 24000000 | tf_op jit(solution)/shard_map/middle/pallas_call | solution.py:36
  38.0 1.6 %collective-permute-start.2 = (bf16[4,1024]{1,0:T(4,128)(2,1)S(1)}, bf16[4,1024]{1,0:T(4,128)(2,1)S(1)}, u32[]{:S(2)}, u32[]{:S(2)}) collective-permute-start(bf16[4,1024]{1,0:T(4,128)(2,1)S(1)} %get-tuple-element.27), channel_id=1, source_target_pairs={{1,0},{0,1},{3,2},{2,3},{5,4},{4,5},{7,6},{6,7},{9,8},{8,9},{11,10... | collective-permute-start | bytes 24584 | tf_op jit(solution)/shard_map/back/ppermute | solution.py:213
  39.6 4.1 %last.1 = (bf16[4,1024,1024]{2,1,0:T(8,128)(2,1)}, bf16[216,1024]{1,0:T(8,128)(2,1)}, f32[4,1024]{1,0:T(4,128)S(1)}) custom-call(bf16[4,1024]{1,0:T(4,128)(2,1)S(1)} %get-tuple-element.18.refs_0_.refs_2_, bf16[4,1024]{1,0:T(4,128)(2,1)S(1)} %collective-permute-done.refs_1_.refs_3_, bf16[4,2,1024]{2,1,0:T(2,128)(2,1)S(1)} %get-tuple-element.22.refs_2_, ...), custom_call_target="tpu_custom_call" | custom-call | flops 4000000000 | bytes 15000000 | tf_op jit(solution)/shard_map/ending/last/pallas_call | solution.py:36
  43.7 0.0 collective-permute-done.2
  43.7 0.6 %add_bitcast_fusion = f32[1,4,1024]{2,1,0:T(4,128)} fusion(f32[4,1024]{1,0:T(4,128)S(1)} %get-tuple-element.26, bf16[4,1024]{1,0:T(4,128)(2,1)S(1)} %collective-permute-done.2), kind=kLoop, calls=%fused_computation | loop fusion | flops 8192 | bytes 40960 | tf_op jit(solution)/shard_map/broadcast_in_dim | solution.py:270
  (4 shorter events, 0.0 us)
Async XLA Ops:
  2.9 19.6 %all-to-all-start = ((bf16[48,4,1024]{2,1,0:T(4,128)(2,1)}), bf16[48,4,1024]{2,1,0:T(4,128)(2,1)S(1)}, u32[]{:S(2)}, u32[]{:S(2)}) async-start(bf16[48,4,1024]{2,1,0:T(4,128)(2,1)} %get-tuple-element.19), calls=%async_computation | async-start | bytes 786432 | tf_op jit(solution)/shard_map/all_to_all | solution.py:238
  10.3 3.7 %collective-permute-start = (bf16[4,1024]{1,0:T(4,128)(2,1)S(1)}, bf16[4,1024]{1,0:T(4,128)(2,1)S(1)}, u32[]{:S(2)}, u32[]{:S(2)}) collective-permute-start(bf16[4,1024]{1,0:T(4,128)(2,1)S(1)} %get-tuple-element.18.refs_0_.refs_2_), channel_id=1, source_target_pairs={{1,0},{0,1},{3,2},{2,3},{5,4},{4,5},{7,6},{6,7},{9,8},{8,9},{11,10... | collective-permute-start | bytes 24584 | tf_op jit(solution)/shard_map/ppermute | solution.py:213
  22.5 3.8 %slice-start = ((s8[8388608]{0:T(1024)(128)(4,1)}), s8[4194304]{0:T(1024)(128)(4,1)S(1)}, s32[]{:S(2)}) async-start(s8[8388608]{0:T(1024)(128)(4,1)} %bitcast.9), calls=%async_computation.1 | async-start | bytes 8388608
  22.5 3.8 %slice-start.2 = ((s8[8388608]{0:T(1024)(128)(4,1)}), s8[4194304]{0:T(1024)(128)(4,1)S(1)}, s32[]{:S(2)}) async-start(s8[8388608]{0:T(1024)(128)(4,1)} %bitcast.11), calls=%async_computation.3 | async-start | bytes 8388608
  22.5 4.6 %slice-start.1 = ((s8[8388608]{0:T(1024)(128)(4,1)}), s8[4194304]{0:T(1024)(128)(4,1)S(1)}, s32[]{:S(2)}) async-start(s8[8388608]{0:T(1024)(128)(4,1)} %bitcast.9), calls=%async_computation.2 | async-start | bytes 8388608
  22.5 5.8 %slice-start.3 = ((s8[8388608]{0:T(1024)(128)(4,1)}), s8[4194304]{0:T(1024)(128)(4,1)S(1)}, s32[]{:S(2)}) async-start(s8[8388608]{0:T(1024)(128)(4,1)} %bitcast.11), calls=%async_computation.4 | async-start | bytes 8388608
  22.5 3.7 %collective-permute-start.1 = (bf16[4,1024]{1,0:T(4,128)(2,1)S(1)}, bf16[4,1024]{1,0:T(4,128)(2,1)S(1)}, u32[]{:S(2)}, u32[]{:S(2)}) collective-permute-start(bf16[4,1024]{1,0:T(4,128)(2,1)S(1)} %sum.1.x_ref), channel_id=1, source_target_pairs={{1,0},{0,1},{3,2},{2,3},{5,4},{4,5},{7,6},{6,7},{9,8},{8,9},{11,10... | collective-permute-start | bytes 24584 | tf_op jit(solution)/shard_map/ppermute | solution.py:213
  38.0 5.7 %collective-permute-start.2 = (bf16[4,1024]{1,0:T(4,128)(2,1)S(1)}, bf16[4,1024]{1,0:T(4,128)(2,1)S(1)}, u32[]{:S(2)}, u32[]{:S(2)}) collective-permute-start(bf16[4,1024]{1,0:T(4,128)(2,1)S(1)} %get-tuple-element.27), channel_id=1, source_target_pairs={{1,0},{0,1},{3,2},{2,3},{5,4},{4,5},{7,6},{6,7},{9,8},{8,9},{11,10... | collective-permute-start | bytes 24584 | tf_op jit(solution)/shard_map/back/ppermute | solution.py:213

commit v4 on v3

--- a/solution.py
+++ b/solution.py
@@ -74,14 +74,17 @@
 
 def forward_kernel(n_grp, *refs):
     x_refs = refs[:n_grp]
-    w_gate_hbm, w_up_hbm, gate_ref, up_ref, w_gate_ref, w_up_ref, sems = refs[n_grp:]
+    w_gate_hbm, w_up_hbm, gate_ref, up_ref, first_ref, w_gate_ref, w_up_ref, sems = refs[n_grp:]
     experts = gate_ref.shape[0]
-    pairs = ((w_gate_hbm, w_gate_ref), (w_up_hbm, w_up_ref))
-    copies = [[start(s.at[e], d.at[e], sems.at[i, e]) for i, (s, d) in enumerate(pairs)] for e in range(experts)]
+    gates = [first_ref.at[0]] + [w_gate_ref.at[e] for e in range(experts - 1)]
+    copies = []
+    for e in range(experts):
+        one = start(w_gate_hbm.at[e], gates[e], sems.at[0, e])
+        copies.append((one, start(w_up_hbm.at[e], w_up_ref.at[e], sems.at[1, e])))
     for e in range(experts):
         x = jnp.concatenate([r[e : e + 1] for r in x_refs], axis=0)
         copies[e][0].wait()
-        gate_ref[e] = dot(x, w_gate_ref[e], ((1,), (1,)))
+        gate_ref[e] = dot(x, gates[e][...], ((1,), (1,)))
         copies[e][1].wait()
         up_ref[e] = dot(x, w_up_ref[e], ((1,), (1,)))
 
@@ -138,16 +141,16 @@
 
 def middle_kernel(n_grp, *refs):
     so_refs, x_refs = refs[:n_grp], refs[n_grp : 2 * n_grp]
-    gate_ref, up_ref, w_gate_hbm, w_up_ref, w_down_ref = refs[2 * n_grp : 2 * n_grp + 5]
-    partial_refs = refs[2 * n_grp + 5 : 3 * n_grp + 5]
+    gate_ref, up_ref, w_gate_hbm, w_up_ref, w_down_ref, first_ref = refs[2 * n_grp : 2 * n_grp + 6]
+    partial_refs = refs[2 * n_grp + 6 : 3 * n_grp + 6]
     (up_grad_ref, grad_down_hbm, grad_gate_hbm, so_ref, x_ref, sum_ref, w_gate_ref, down_buf, gate_buf,
-     w_gate_sems, down_sems, gate_sems) = refs[3 * n_grp + 5 :]
+     w_gate_sems, down_sems, gate_sems) = refs[3 * n_grp + 6 :]
     experts = gate_ref.shape[0]
 
     def w_gate_copy(e):
-        return pltpu.make_async_copy(w_gate_hbm.at[e], w_gate_ref.at[e], w_gate_sems.at[e])
-
-    for e in range(experts):
+        return pltpu.make_async_copy(w_gate_hbm.at[e], w_gate_ref.at[e - 1], w_gate_sems.at[e - 1])
+
+    for e in range(1, experts):
         w_gate_copy(e).start()
     stack_rows(so_refs, so_ref)
     stack_rows(x_refs, x_ref)
@@ -156,7 +159,9 @@
         return dot(so_ref[e], w_down_ref[e], ((1,), (1,)))
 
     def step(e, hidden_grad):
-        w_gate_copy(e).wait()
+        if e > 0:
+            w_gate_copy(e).wait()
+        w_gate = first_ref[0] if e == 0 else w_gate_ref[e - 1]
         gate, up = gate_ref[e], up_ref[e]
         sig = 1.0 / (1.0 + jnp.exp(-gate))
         hidden = (gate * sig * up).astype(BF16)
@@ -164,7 +169,7 @@
         gate_grad = (hidden_grad * up * sig * (1.0 + gate * (1.0 - sig))).astype(BF16)
         up_grad_ref[e] = up_grad
         later = hidden_grad_of(min(e + 1, experts - 1))
-        sum_ref[e] = dot(gate_grad, w_gate_ref[e], ((1,), (0,))) + dot(up_grad, w_up_ref[e], ((1,), (0,)))
+        sum_ref[e] = dot(gate_grad, w_gate, ((1,), (0,))) + dot(up_grad, w_up_ref[e], ((1,), (0,)))
         outer_into(hidden.astype(F32), so_ref[e].astype(F32), down_buf, e)
         outer_into(gate_grad.astype(F32), x_ref[e].astype(F32), gate_buf, e)
         send(down_buf, grad_down_hbm, down_sems, e)
@@ -237,9 +242,11 @@
     )
     every = lax.all_to_all(partial, "seq", split_axis=0, concat_axis=0, tiled=True)
     inputs = [x_own] + [shifted(x_own, n_grp, k) for k in range(1, n_grp)]
-    gate, up = call(
-        functools.partial(forward_kernel, n_grp), "forward", (shape(vec, F32), shape(vec, F32)), (VMEM, VMEM),
-        (*inputs, in_hbm(w_gate), in_hbm(w_up)), (VMEM,) * n_grp + (HBM, HBM), scratch=(buf, buf, SEMS((2, own))),
+    gate, up, w_first = call(
+        functools.partial(forward_kernel, n_grp), "forward",
+        (shape(vec, F32), shape(vec, F32), pltpu.VMEM((1, rows, width), BF16)), (VMEM,) * 3,
+        (*inputs, in_hbm(w_gate), in_hbm(w_up)), (VMEM,) * n_grp + (HBM, HBM),
+        scratch=(pltpu.VMEM((own - 1, rows, width), BF16), buf, SEMS((2, own))),
         us=6, vmem=24 << 20,
     )
     slot_out = call(sum_kernel, "sum", shape((own, width), BF16), VMEM, (every, gate), (VMEM, VMEM), us=20)
@@ -249,10 +256,10 @@
         functools.partial(middle_kernel, n_grp), "middle",
         (shape((own, width), F32),) + (shape((own, width), BF16),) * (n_grp - 1) + (shape(vec, BF16), big, big),
         (VMEM,) * (n_grp + 1) + (HBM, HBM),
-        (*all_out, *inputs, gate, up, in_hbm(w_gate), w_up, w_down),
-        (VMEM,) * (2 * n_grp + 2) + (HBM, VMEM, VMEM),
-        scratch=(few, few, pltpu.VMEM((own, n_grp, width), F32), buf, buf, buf,
-                 SEMS((own,)), sems, sems),
+        (*all_out, *inputs, gate, up, in_hbm(w_gate), w_up, w_down, w_first),
+        (VMEM,) * (2 * n_grp + 2) + (HBM, VMEM, VMEM, VMEM),
+        scratch=(few, few, pltpu.VMEM((own, n_grp, width), F32), pltpu.VMEM((own - 1, rows, width), BF16),
+                 buf, buf, SEMS((own - 1,)), sems, sems),
         us=8, vmem=32 << 20,
     )
     with jax.named_scope("back"):

time: 44.6 us -> 43.3 us (0.971)
  Pallas kernels: 23 us -> 21.8 us
    pallas_call x6, Pallas kernels: 23 us -> 21.8 us  [call(): pl.pallas_call(body, name=name, out_shape=outs, in_specs=in_specs, out_sp...]
  transfers between devices with their start and end apart: 4 -> 4, of which waited for: 3 -> 3; matrix products, arithmetic and copies ran while one was open for 0% -> 0% of each run, Pallas kernels for 25% -> 26%
where the time goes in v4:
time: 43.3 us; the launch traced here: 43.1 us
  Pallas kernels  21.8 us (50%)
  starting transfers between devices  12.2 us (28%)
  waiting for transfers between devices  5.73 us (13%)
  local copies, waits for them, and re-layouts  2.1 us (5%)
  between operations  0.7 us (2%)
  other arithmetic  0.61 us (1%)
    pallas_call x6, Pallas kernels, call(): pl.pallas_call(body, name=name, out_shape=outs, in_specs=in_specs, out_sp...  21.8 us
    all_to_all x1, starting transfers between devices, per_device(): lax.all_to_all(partial, 'seq', split_axis=0, concat_axis=0, tiled=True)  7.4 us
    ppermute x3, starting transfers between devices, shifted(): return lax.ppermute(x, 'grp', [((i + k) % size, i) for i in range(size)])  4.75 us
    ppermute x3, waiting for transfers between devices, shifted(): return lax.ppermute(x, 'grp', [((i + k) % size, i) for i in range(size)])  4.26 us
    unnamed x8, local copies, waits for them, and re-layouts  2.1 us
    all_to_all x1, waiting for transfers between devices, per_device(): lax.all_to_all(partial, 'seq', split_axis=0, concat_axis=0, tiled=True)  1.47 us
  transfers between devices with their start and end apart: 4, of which 3 were waited for; matrix products, arithmetic and copies ran while one was open for 0% of the time, Pallas kernels for 26%

profile of v4, /device:TPU:0, one launch (start us, length us, event | category | flops | bytes accessed | tf_op | source)
XLA Modules:
  0.0 43.1 jit_solution(173196025772930793)
XLA Ops:
  0.6 2.3 %soft.1 = (f32[64,216]{1,0:T(8,128)S(1)}, bf16[48,4,1024]{2,1,0:T(4,128)(2,1)}, bf16[4,1024]{1,0:T(4,128)(2,1)S(1)}) custom-call(f32[64,216]{1,0:T(8,128)} %bitcast.15, bf16[216,1024]{1,0:T(8,128)(2,1)} %bitcast.13, bf16[4,1024]{1,0:T(4,128)(2,1)} %bitcast.16, bf16[4,1024]{1,0:T(4,128)(2,1)} %router_hbm.1, bf16[4,1024]{1,0:T(4,128)(2,1)} %bitcast.17), custom_call_target="tpu_custom_call" | custom-call | flops 800000000 | bytes 3000000 | tf_op jit(solution)/shard_map/soft/pallas_call | solution.py:36
  2.9 7.4 %all-to-all-start = ((bf16[48,4,1024]{2,1,0:T(4,128)(2,1)}), bf16[48,4,1024]{2,1,0:T(4,128)(2,1)S(1)}, u32[]{:S(2)}, u32[]{:S(2)}) async-start(bf16[48,4,1024]{2,1,0:T(4,128)(2,1)} %get-tuple-element.20), calls=%async_computation | async-start | bytes 786432 | tf_op jit(solution)/shard_map/all_to_all | solution.py:243
  10.3 1.6 %collective-permute-start = (bf16[4,1024]{1,0:T(4,128)(2,1)S(1)}, bf16[4,1024]{1,0:T(4,128)(2,1)S(1)}, u32[]{:S(2)}, u32[]{:S(2)}) collective-permute-start(bf16[4,1024]{1,0:T(4,128)(2,1)S(1)} %get-tuple-element.19.refs_0_.refs_2_), channel_id=1, source_target_pairs={{1,0},{0,1},{3,2},{2,3},{5,4},{4,5},{7,6},{6,7},{9,8},{8,9},{11,10... | collective-permute-start | bytes 24584 | tf_op jit(solution)/shard_map/ppermute | solution.py:218
  11.9 2.1 %collective-permute-done.refs_1_.refs_3_ = bf16[4,1024]{1,0:T(4,128)(2,1)S(1)} collective-permute-done((bf16[4,1024]{1,0:T(4,128)(2,1)S(1)}, bf16[4,1024]{1,0:T(4,128)(2,1)S(1)}, u32[]{:S(2)}, u32[]{:S(2)}) %collective-permute-start) | collective-permute-done | bytes 8224 | tf_op jit(solution)/shard_map/ppermute | solution.py:218
  14.0 7.0 %forward.1 = (f32[4,2,1024]{2,1,0:T(2,128)S(1)}, f32[4,2,1024]{2,1,0:T(2,128)S(1)}, bf16[1,1024,1024]{2,1,0:T(8,128)(2,1)S(1)}) custom-call(bf16[4,1024]{1,0:T(4,128)(2,1)S(1)} %get-tuple-element.19.refs_0_.refs_2_, bf16[4,1024]{1,0:T(4,128)(2,1)S(1)} %collective-permute-done.refs_1_.refs_3_, bf16[4,1024,1024]{2,1,0:T(8,128)(2,1)} %refs_6_.1, ...), custom_call_target="tpu_custom_call" | custom-call | flops 4800000000 | bytes 18000000 | tf_op jit(solution)/shard_map/forward/pallas_call | solution.py:36
  21.0 1.5 %all-to-all-done.every_ref.refs_5_ = bf16[48,4,1024]{2,1,0:T(4,128)(2,1)S(1)} async-done(((bf16[48,4,1024]{2,1,0:T(4,128)(2,1)}), bf16[48,4,1024]{2,1,0:T(4,128)(2,1)S(1)}, u32[]{:S(2)}, u32[]{:S(2)}) %all-to-all-start) | async-done | bytes 393248 | tf_op jit(solution)/shard_map/all_to_all | solution.py:243
  22.5 0.0 slice-start
  22.5 0.0 slice-start.2
  22.5 0.0 slice-start.1
  22.5 0.0 slice-start.3
  22.5 1.6 %collective-permute-start.1 = (bf16[4,1024]{1,0:T(4,128)(2,1)S(1)}, bf16[4,1024]{1,0:T(4,128)(2,1)S(1)}, u32[]{:S(2)}, u32[]{:S(2)}) collective-permute-start(bf16[4,1024]{1,0:T(4,128)(2,1)S(1)} %sum.1.x_ref), channel_id=1, source_target_pairs={{1,0},{0,1},{3,2},{2,3},{5,4},{4,5},{7,6},{6,7},{9,8},{8,9},{11,10... | collective-permute-start | bytes 24584 | tf_op jit(solution)/shard_map/ppermute | solution.py:218
  24.1 2.1 %collective-permute-done.1.refs_1_ = bf16[4,1024]{1,0:T(4,128)(2,1)S(1)} collective-permute-done((bf16[4,1024]{1,0:T(4,128)(2,1)S(1)}, bf16[4,1024]{1,0:T(4,128)(2,1)S(1)}, u32[]{:S(2)}, u32[]{:S(2)}) %collective-permute-start.1) | collective-permute-done | bytes 8224 | tf_op jit(solution)/shard_map/ppermute | solution.py:218
  26.3 0.0 slice-done
  26.3 0.0 slice-done.2
  26.3 0.9 %slice-done.1 = s8[4194304]{0:T(1024)(128)(4,1)S(1)} async-done(((s8[8388608]{0:T(1024)(128)(4,1)}), s8[4194304]{0:T(1024)(128)(4,1)S(1)}, s32[]{:S(2)}) %slice-start.1) | async-done | bytes 4194328
  27.2 1.2 %slice-done.3 = s8[4194304]{0:T(1024)(128)(4,1)S(1)} async-done(((s8[8388608]{0:T(1024)(128)(4,1)}), s8[4194304]{0:T(1024)(128)(4,1)S(1)}, s32[]{:S(2)}) %slice-start.3) | async-done | bytes 4194328
  28.4 8.4 %middle.1 = (f32[4,1024]{1,0:T(4,128)S(1)}, bf16[4,1024]{1,0:T(4,128)(2,1)S(1)}, bf16[4,2,1024]{2,1,0:T(2,128)(2,1)S(1)}, bf16[4,1024,1024]{2,1,0:T(8,128)(2,1)}, bf16[4,1024,1024]{2,1,0:T(8,128)(2,1)}) custom-call(bf16[4,1024]{1,0:T(4,128)(2,1)S(1)} %pause.1.refs_0_, bf16[4,1024]{1,0:T(4,128)(2,1)S(1)} %collective-permute-done.1.refs_1_, ...), custom_call_target="tpu_custom_call" | custom-call | flops 6400000000 | bytes 24000000 | tf_op jit(solution)/shard_map/middle/pallas_call | solution.py:36
  36.7 1.6 %collective-permute-start.2 = (bf16[4,1024]{1,0:T(4,128)(2,1)S(1)}, bf16[4,1024]{1,0:T(4,128)(2,1)S(1)}, u32[]{:S(2)}, u32[]{:S(2)}) collective-permute-start(bf16[4,1024]{1,0:T(4,128)(2,1)S(1)} %get-tuple-element.29), channel_id=1, source_target_pairs={{1,0},{0,1},{3,2},{2,3},{5,4},{4,5},{7,6},{6,7},{9,8},{8,9},{11,10... | collective-permute-start | bytes 24584 | tf_op jit(solution)/shard_map/back/ppermute | solution.py:218
  38.3 4.1 %last.1 = (bf16[4,1024,1024]{2,1,0:T(8,128)(2,1)}, bf16[216,1024]{1,0:T(8,128)(2,1)}, f32[4,1024]{1,0:T(4,128)S(1)}) custom-call(bf16[4,1024]{1,0:T(4,128)(2,1)S(1)} %get-tuple-element.19.refs_0_.refs_2_, bf16[4,1024]{1,0:T(4,128)(2,1)S(1)} %collective-permute-done.refs_1_.refs_3_, bf16[4,2,1024]{2,1,0:T(2,128)(2,1)S(1)} %get-tuple-element.24.refs_2_, ...), custom_call_target="tpu_custom_call" | custom-call | flops 4000000000 | bytes 15000000 | tf_op jit(solution)/shard_map/ending/last/pallas_call | solution.py:36
  42.5 0.0 collective-permute-done.2
  42.5 0.6 %add_bitcast_fusion = f32[1,4,1024]{2,1,0:T(4,128)} fusion(f32[4,1024]{1,0:T(4,128)S(1)} %get-tuple-element.28, bf16[4,1024]{1,0:T(4,128)(2,1)S(1)} %collective-permute-done.2), kind=kLoop, calls=%fused_computation | loop fusion | flops 8192 | bytes 40960 | tf_op jit(solution)/shard_map/broadcast_in_dim | solution.py:277
  (4 shorter events, 0.0 us)
Async XLA Ops:
  2.9 19.6 %all-to-all-start = ((bf16[48,4,1024]{2,1,0:T(4,128)(2,1)}), bf16[48,4,1024]{2,1,0:T(4,128)(2,1)S(1)}, u32[]{:S(2)}, u32[]{:S(2)}) async-start(bf16[48,4,1024]{2,1,0:T(4,128)(2,1)} %get-tuple-element.20), calls=%async_computation | async-start | bytes 786432 | tf_op jit(solution)/shard_map/all_to_all | solution.py:243
  10.3 3.7 %collective-permute-start = (bf16[4,1024]{1,0:T(4,128)(2,1)S(1)}, bf16[4,1024]{1,0:T(4,128)(2,1)S(1)}, u32[]{:S(2)}, u32[]{:S(2)}) collective-permute-start(bf16[4,1024]{1,0:T(4,128)(2,1)S(1)} %get-tuple-element.19.refs_0_.refs_2_), channel_id=1, source_target_pairs={{1,0},{0,1},{3,2},{2,3},{5,4},{4,5},{7,6},{6,7},{9,8},{8,9},{11,10... | collective-permute-start | bytes 24584 | tf_op jit(solution)/shard_map/ppermute | solution.py:218
  22.5 3.8 %slice-start = ((s8[8388608]{0:T(1024)(128)(4,1)}), s8[4194304]{0:T(1024)(128)(4,1)S(1)}, s32[]{:S(2)}) async-start(s8[8388608]{0:T(1024)(128)(4,1)} %bitcast.9), calls=%async_computation.1 | async-start | bytes 8388608
  22.5 3.8 %slice-start.2 = ((s8[8388608]{0:T(1024)(128)(4,1)}), s8[4194304]{0:T(1024)(128)(4,1)S(1)}, s32[]{:S(2)}) async-start(s8[8388608]{0:T(1024)(128)(4,1)} %bitcast.11), calls=%async_computation.3 | async-start | bytes 8388608
  22.5 4.6 %slice-start.1 = ((s8[8388608]{0:T(1024)(128)(4,1)}), s8[4194304]{0:T(1024)(128)(4,1)S(1)}, s32[]{:S(2)}) async-start(s8[8388608]{0:T(1024)(128)(4,1)} %bitcast.9), calls=%async_computation.2 | async-start | bytes 8388608
  22.5 5.8 %slice-start.3 = ((s8[8388608]{0:T(1024)(128)(4,1)}), s8[4194304]{0:T(1024)(128)(4,1)S(1)}, s32[]{:S(2)}) async-start(s8[8388608]{0:T(1024)(128)(4,1)} %bitcast.11), calls=%async_computation.4 | async-start | bytes 8388608
  22.5 3.7 %collective-permute-start.1 = (bf16[4,1024]{1,0:T(4,128)(2,1)S(1)}, bf16[4,1024]{1,0:T(4,128)(2,1)S(1)}, u32[]{:S(2)}, u32[]{:S(2)}) collective-permute-start(bf16[4,1024]{1,0:T(4,128)(2,1)S(1)} %sum.1.x_ref), channel_id=1, source_target_pairs={{1,0},{0,1},{3,2},{2,3},{5,4},{4,5},{7,6},{6,7},{9,8},{8,9},{11,10... | collective-permute-start | bytes 24584 | tf_op jit(solution)/shard_map/ppermute | solution.py:218
  36.7 5.7 %collective-permute-start.2 = (bf16[4,1024]{1,0:T(4,128)(2,1)S(1)}, bf16[4,1024]{1,0:T(4,128)(2,1)S(1)}, u32[]{:S(2)}, u32[]{:S(2)}) collective-permute-start(bf16[4,1024]{1,0:T(4,128)(2,1)S(1)} %get-tuple-element.29), channel_id=1, source_target_pairs={{1,0},{0,1},{3,2},{2,3},{5,4},{4,5},{7,6},{6,7},{9,8},{8,9},{11,10... | collective-permute-start | bytes 24584 | tf_op jit(solution)/shard_map/back/ppermute | solution.py:218

commit v5 on v4

--- a/solution.py
+++ b/solution.py
@@ -45,8 +45,8 @@
     )(*args)
 
 
-def soft_kernel(logits_hbm, grads_hbm, outputs_hbm, router_hbm, x_hbm, probs_ref, all_hbm, x_ref,
-                logits_ref, grads_ref, both_ref, parts_ref, sems, both_sems, parts_sems):
+def soft_kernel(logits_hbm, grads_hbm, outputs_hbm, router_hbm, x_hbm, probs_ref, all_hbm, x_ref, grads_ref,
+                logits_ref, both_ref, parts_ref, sems, both_sems, parts_sems):
     loads = [
         start(outputs_hbm, both_ref.at[0], sems.at[2]),
         start(router_hbm, both_ref.at[1], sems.at[3]),
@@ -188,10 +188,9 @@
 
 def last_kernel(n_grp, *refs):
     x_refs = refs[:n_grp]
-    (up_grad_ref, probs_ref, grads_hbm, every_ref, partial_ref, grad_up_hbm, token_hbm, same_ref,
-     x_ref, up_buf, grads_ref, token_ref, up_sems, sems) = refs[n_grp:]
+    (up_grad_ref, probs_ref, grads_ref, every_ref, partial_ref, grad_up_hbm, token_hbm, same_ref,
+     x_ref, up_buf, token_ref, up_sems, sems) = refs[n_grp:]
     experts = up_grad_ref.shape[0]
-    loaded = start(grads_hbm, grads_ref, sems.at[0])
     same_ref[...] = partial_ref[...]
     stack_rows(x_refs, x_ref)
 
@@ -204,7 +203,6 @@
     n = every_ref.shape[0] // 3
     outputs = jnp.concatenate([every_ref[3 * j + 1] for j in range(n)], axis=0)
     routers = jnp.concatenate([every_ref[3 * j + 2] for j in range(n)], axis=0)
-    loaded.wait()
     weight_grad = dot(outputs, grads_ref[...], ((1,), (1,)))
     centre = jnp.sum(weight_grad * probs, axis=0, keepdims=True)
     logit_grad = (probs * (weight_grad - centre)).astype(BF16)
@@ -224,7 +222,7 @@
     rows = w_gate.shape[1]
     tokens = grads.shape[0]
     slots = n_seq * own
-    block = min(256, rows)
+    block = min(512, rows)
     vec = (own, n_grp, rows)
     held = pltpu.VMEM((own, rows, width), BF16)
     big = shape((own, rows, width), BF16)
@@ -232,12 +230,13 @@
     few = pltpu.VMEM((own, n_grp, width), BF16)
     held_tokens = pltpu.VMEM((tokens, width), BF16)
     sems = SEMS((own, rows // block))
-    probs, partial, x_own = call(
+    probs, partial, x_own, grads_v = call(
         soft_kernel, "soft",
-        (shape((slots, tokens), F32), shape((3 * n_seq, own, width), BF16), shape((own, width), BF16)),
-        (VMEM, HBM, VMEM),
+        (shape((slots, tokens), F32), shape((3 * n_seq, own, width), BF16), shape((own, width), BF16),
+         pltpu.VMEM((tokens, width), BF16)),
+        (VMEM, HBM, VMEM, VMEM),
         tuple(map(in_hbm, (combine_logits[0].T, grads, expert_out[0], router, slot_in[0]))), (HBM,) * 5,
-        scratch=(pltpu.VMEM((slots, tokens), F32), held_tokens, pltpu.VMEM((2, own, width), BF16),
+        scratch=(pltpu.VMEM((slots, tokens), F32), pltpu.VMEM((2, own, width), BF16),
                  pltpu.VMEM((n_seq, own, width), BF16), SEMS((5,)), SEMS((n_seq,)), SEMS((n_seq,))),
     )
     every = lax.all_to_all(partial, "seq", split_axis=0, concat_axis=0, tiled=True)
@@ -268,9 +267,9 @@
         grad_up, token_grad, slot_grad = call(
             functools.partial(last_kernel, n_grp), "last",
             (big, shape((tokens, width), BF16), shape((own, width), F32)), (HBM, HBM, VMEM),
-            (*inputs, up_grad, probs, in_hbm(grads), every, partials[0]),
-            (VMEM,) * (n_grp + 2) + (HBM, VMEM, VMEM),
-            scratch=(few, buf, held_tokens, held_tokens, sems, SEMS((2,))), us=5, vmem=24 << 20,
+            (*inputs, up_grad, probs, grads_v, every, partials[0]),
+            (VMEM,) * (n_grp + 5),
+            scratch=(few, buf, held_tokens, sems, SEMS((2,))), us=5, vmem=24 << 20,
         )
     for part in back:
         slot_grad = slot_grad + part.astype(F32)

time: 43.3 us -> 43.1 us (level)
  no operation moved by 1% of the time
where the time goes in v5:
time: 43.1 us; the launch traced here: 42.9 us
  Pallas kernels  21.6 us (50%)
  starting transfers between devices  12.2 us (28%)
  waiting for transfers between devices  5.73 us (13%)
  local copies, waits for them, and re-layouts  2.1 us (5%)
  between operations  0.7 us (2%)
  other arithmetic  0.61 us (1%)
    pallas_call x6, Pallas kernels, call(): pl.pallas_call(body, name=name, out_shape=outs, in_specs=in_specs, out_sp...  21.6 us
    all_to_all x1, starting transfers between devices, per_device(): lax.all_to_all(partial, 'seq', split_axis=0, concat_axis=0, tiled=True)  7.4 us
    ppermute x3, starting transfers between devices, shifted(): return lax.ppermute(x, 'grp', [((i + k) % size, i) for i in range(size)])  4.75 us
    ppermute x3, waiting for transfers between devices, shifted(): return lax.ppermute(x, 'grp', [((i + k) % size, i) for i in range(size)])  4.26 us
    unnamed x8, local copies, waits for them, and re-layouts  2.1 us
    all_to_all x1, waiting for transfers between devices, per_device(): lax.all_to_all(partial, 'seq', split_axis=0, concat_axis=0, tiled=True)  1.47 us
  transfers between devices with their start and end apart: 4, of which 3 were waited for; matrix products, arithmetic and copies ran while one was open for 0% of the time, Pallas kernels for 26%

profile of v5, /device:TPU:0, one launch (start us, length us, event | category | flops | bytes accessed | tf_op | source)
XLA Modules:
  0.0 42.9 jit_solution(15923863847995450488)
XLA Ops:
  0.6 2.3 %soft.1 = (f32[64,216]{1,0:T(8,128)S(1)}, bf16[48,4,1024]{2,1,0:T(4,128)(2,1)}, bf16[4,1024]{1,0:T(4,128)(2,1)S(1)}, bf16[216,1024]{1,0:T(8,128)(2,1)S(1)}) custom-call(f32[64,216]{1,0:T(8,128)} %bitcast.14, bf16[216,1024]{1,0:T(8,128)(2,1)} %bitcast.13, bf16[4,1024]{1,0:T(4,128)(2,1)} %bitcast.15, bf16[4,1024]{1,0:T(4,128)(2,1)} %router_hbm.1, ...), custom_call_target="tpu_custom_call" | custom-call | flops 800000000 | bytes 3000000 | tf_op jit(solution)/shard_map/soft/pallas_call | solution.py:36
  2.9 7.4 %all-to-all-start = ((bf16[48,4,1024]{2,1,0:T(4,128)(2,1)}), bf16[48,4,1024]{2,1,0:T(4,128)(2,1)S(1)}, u32[]{:S(2)}, u32[]{:S(2)}) async-start(bf16[48,4,1024]{2,1,0:T(4,128)(2,1)} %get-tuple-element.21), calls=%async_computation | async-start | bytes 786432 | tf_op jit(solution)/shard_map/all_to_all | solution.py:242
  10.3 1.6 %collective-permute-start = (bf16[4,1024]{1,0:T(4,128)(2,1)S(1)}, bf16[4,1024]{1,0:T(4,128)(2,1)S(1)}, u32[]{:S(2)}, u32[]{:S(2)}) collective-permute-start(bf16[4,1024]{1,0:T(4,128)(2,1)S(1)} %get-tuple-element.20.refs_0_.refs_2_), channel_id=1, source_target_pairs={{1,0},{0,1},{3,2},{2,3},{5,4},{4,5},{7,6},{6,7},{9,8},{8,9},{11,10... | collective-permute-start | bytes 24584 | tf_op jit(solution)/shard_map/ppermute | solution.py:216
  11.9 2.1 %collective-permute-done.refs_1_.refs_3_ = bf16[4,1024]{1,0:T(4,128)(2,1)S(1)} collective-permute-done((bf16[4,1024]{1,0:T(4,128)(2,1)S(1)}, bf16[4,1024]{1,0:T(4,128)(2,1)S(1)}, u32[]{:S(2)}, u32[]{:S(2)}) %collective-permute-start) | collective-permute-done | bytes 8224 | tf_op jit(solution)/shard_map/ppermute | solution.py:216
  14.0 7.0 %forward.1 = (f32[4,2,1024]{2,1,0:T(2,128)S(1)}, f32[4,2,1024]{2,1,0:T(2,128)S(1)}, bf16[1,1024,1024]{2,1,0:T(8,128)(2,1)S(1)}) custom-call(bf16[4,1024]{1,0:T(4,128)(2,1)S(1)} %get-tuple-element.20.refs_0_.refs_2_, bf16[4,1024]{1,0:T(4,128)(2,1)S(1)} %collective-permute-done.refs_1_.refs_3_, bf16[4,1024,1024]{2,1,0:T(8,128)(2,1)} %refs_6_.1, ...), custom_call_target="tpu_custom_call" | custom-call | flops 4800000000 | bytes 18000000 | tf_op jit(solution)/shard_map/forward/pallas_call | solution.py:36
  21.0 1.5 %all-to-all-done.every_ref.refs_5_ = bf16[48,4,1024]{2,1,0:T(4,128)(2,1)S(1)} async-done(((bf16[48,4,1024]{2,1,0:T(4,128)(2,1)}), bf16[48,4,1024]{2,1,0:T(4,128)(2,1)S(1)}, u32[]{:S(2)}, u32[]{:S(2)}) %all-to-all-start) | async-done | bytes 393248 | tf_op jit(solution)/shard_map/all_to_all | solution.py:242
  22.5 0.0 slice-start
  22.5 0.0 slice-start.2
  22.5 0.0 slice-start.1
  22.5 0.0 slice-start.3
  22.5 1.6 %collective-permute-start.1 = (bf16[4,1024]{1,0:T(4,128)(2,1)S(1)}, bf16[4,1024]{1,0:T(4,128)(2,1)S(1)}, u32[]{:S(2)}, u32[]{:S(2)}) collective-permute-start(bf16[4,1024]{1,0:T(4,128)(2,1)S(1)} %sum.1.x_ref), channel_id=1, source_target_pairs={{1,0},{0,1},{3,2},{2,3},{5,4},{4,5},{7,6},{6,7},{9,8},{8,9},{11,10... | collective-permute-start | bytes 24584 | tf_op jit(solution)/shard_map/ppermute | solution.py:216
  24.1 2.1 %collective-permute-done.1.refs_1_ = bf16[4,1024]{1,0:T(4,128)(2,1)S(1)} collective-permute-done((bf16[4,1024]{1,0:T(4,128)(2,1)S(1)}, bf16[4,1024]{1,0:T(4,128)(2,1)S(1)}, u32[]{:S(2)}, u32[]{:S(2)}) %collective-permute-start.1) | collective-permute-done | bytes 8224 | tf_op jit(solution)/shard_map/ppermute | solution.py:216
  26.3 0.0 slice-done
  26.3 0.0 slice-done.2
  26.3 0.9 %slice-done.1 = s8[4194304]{0:T(1024)(128)(4,1)S(1)} async-done(((s8[8388608]{0:T(1024)(128)(4,1)}), s8[4194304]{0:T(1024)(128)(4,1)S(1)}, s32[]{:S(2)}) %slice-start.1) | async-done | bytes 4194328
  27.2 1.2 %slice-done.3 = s8[4194304]{0:T(1024)(128)(4,1)S(1)} async-done(((s8[8388608]{0:T(1024)(128)(4,1)}), s8[4194304]{0:T(1024)(128)(4,1)S(1)}, s32[]{:S(2)}) %slice-start.3) | async-done | bytes 4194328
  28.4 8.3 %middle.1 = (f32[4,1024]{1,0:T(4,128)S(1)}, bf16[4,1024]{1,0:T(4,128)(2,1)S(1)}, bf16[4,2,1024]{2,1,0:T(2,128)(2,1)S(1)}, bf16[4,1024,1024]{2,1,0:T(8,128)(2,1)}, bf16[4,1024,1024]{2,1,0:T(8,128)(2,1)}) custom-call(bf16[4,1024]{1,0:T(4,128)(2,1)S(1)} %pause.1.refs_0_, bf16[4,1024]{1,0:T(4,128)(2,1)S(1)} %collective-permute-done.1.refs_1_, ...), custom_call_target="tpu_custom_call" | custom-call | flops 6400000000 | bytes 24000000 | tf_op jit(solution)/shard_map/middle/pallas_call | solution.py:36
  36.6 1.6 %collective-permute-start.2 = (bf16[4,1024]{1,0:T(4,128)(2,1)S(1)}, bf16[4,1024]{1,0:T(4,128)(2,1)S(1)}, u32[]{:S(2)}, u32[]{:S(2)}) collective-permute-start(bf16[4,1024]{1,0:T(4,128)(2,1)S(1)} %get-tuple-element.31), channel_id=1, source_target_pairs={{1,0},{0,1},{3,2},{2,3},{5,4},{4,5},{7,6},{6,7},{9,8},{8,9},{11,10... | collective-permute-start | bytes 24584 | tf_op jit(solution)/shard_map/back/ppermute | solution.py:216
  38.2 4.0 %last.1 = (bf16[4,1024,1024]{2,1,0:T(8,128)(2,1)}, bf16[216,1024]{1,0:T(8,128)(2,1)}, f32[4,1024]{1,0:T(4,128)S(1)}) custom-call(bf16[4,1024]{1,0:T(4,128)(2,1)S(1)} %get-tuple-element.20.refs_0_.refs_2_, bf16[4,1024]{1,0:T(4,128)(2,1)S(1)} %collective-permute-done.refs_1_.refs_3_, bf16[4,2,1024]{2,1,0:T(2,128)(2,1)S(1)} %get-tuple-element.25.refs_2_, ...), custom_call_target="tpu_custom_call" | custom-call | flops 4000000000 | bytes 15000000 | tf_op jit(solution)/shard_map/ending/last/pallas_call | solution.py:36
  42.3 0.0 collective-permute-done.2
  42.3 0.6 %add_bitcast_fusion = f32[1,4,1024]{2,1,0:T(4,128)} fusion(f32[4,1024]{1,0:T(4,128)S(1)} %get-tuple-element.30, bf16[4,1024]{1,0:T(4,128)(2,1)S(1)} %collective-permute-done.2), kind=kLoop, calls=%fused_computation | loop fusion | flops 8192 | bytes 40960 | tf_op jit(solution)/shard_map/broadcast_in_dim | solution.py:276
  (4 shorter events, 0.0 us)
Async XLA Ops:
  2.9 19.6 %all-to-all-start = ((bf16[48,4,1024]{2,1,0:T(4,128)(2,1)}), bf16[48,4,1024]{2,1,0:T(4,128)(2,1)S(1)}, u32[]{:S(2)}, u32[]{:S(2)}) async-start(bf16[48,4,1024]{2,1,0:T(4,128)(2,1)} %get-tuple-element.21), calls=%async_computation | async-start | bytes 786432 | tf_op jit(solution)/shard_map/all_to_all | solution.py:242
  10.3 3.7 %collective-permute-start = (bf16[4,1024]{1,0:T(4,128)(2,1)S(1)}, bf16[4,1024]{1,0:T(4,128)(2,1)S(1)}, u32[]{:S(2)}, u32[]{:S(2)}) collective-permute-start(bf16[4,1024]{1,0:T(4,128)(2,1)S(1)} %get-tuple-element.20.refs_0_.refs_2_), channel_id=1, source_target_pairs={{1,0},{0,1},{3,2},{2,3},{5,4},{4,5},{7,6},{6,7},{9,8},{8,9},{11,10... | collective-permute-start | bytes 24584 | tf_op jit(solution)/shard_map/ppermute | solution.py:216
  22.5 3.8 %slice-start = ((s8[8388608]{0:T(1024)(128)(4,1)}), s8[4194304]{0:T(1024)(128)(4,1)S(1)}, s32[]{:S(2)}) async-start(s8[8388608]{0:T(1024)(128)(4,1)} %bitcast.9), calls=%async_computation.1 | async-start | bytes 8388608
  22.5 3.8 %slice-start.2 = ((s8[8388608]{0:T(1024)(128)(4,1)}), s8[4194304]{0:T(1024)(128)(4,1)S(1)}, s32[]{:S(2)}) async-start(s8[8388608]{0:T(1024)(128)(4,1)} %bitcast.11), calls=%async_computation.3 | async-start | bytes 8388608
  22.5 4.6 %slice-start.1 = ((s8[8388608]{0:T(1024)(128)(4,1)}), s8[4194304]{0:T(1024)(128)(4,1)S(1)}, s32[]{:S(2)}) async-start(s8[8388608]{0:T(1024)(128)(4,1)} %bitcast.9), calls=%async_computation.2 | async-start | bytes 8388608
  22.5 5.8 %slice-start.3 = ((s8[8388608]{0:T(1024)(128)(4,1)}), s8[4194304]{0:T(1024)(128)(4,1)S(1)}, s32[]{:S(2)}) async-start(s8[8388608]{0:T(1024)(128)(4,1)} %bitcast.11), calls=%async_computation.4 | async-start | bytes 8388608
  22.5 3.7 %collective-permute-start.1 = (bf16[4,1024]{1,0:T(4,128)(2,1)S(1)}, bf16[4,1024]{1,0:T(4,128)(2,1)S(1)}, u32[]{:S(2)}, u32[]{:S(2)}) collective-permute-start(bf16[4,1024]{1,0:T(4,128)(2,1)S(1)} %sum.1.x_ref), channel_id=1, source_target_pairs={{1,0},{0,1},{3,2},{2,3},{5,4},{4,5},{7,6},{6,7},{9,8},{8,9},{11,10... | collective-permute-start | bytes 24584 | tf_op jit(solution)/shard_map/ppermute | solution.py:216
  36.6 5.6 %collective-permute-start.2 = (bf16[4,1024]{1,0:T(4,128)(2,1)S(1)}, bf16[4,1024]{1,0:T(4,128)(2,1)S(1)}, u32[]{:S(2)}, u32[]{:S(2)}) collective-permute-start(bf16[4,1024]{1,0:T(4,128)(2,1)S(1)} %get-tuple-element.31), channel_id=1, source_target_pairs={{1,0},{0,1},{3,2},{2,3},{5,4},{4,5},{7,6},{6,7},{9,8},{8,9},{11,10... | collective-permute-start | bytes 24584 | tf_op jit(solution)/shard_map/back/ppermute | solution.py:216
